TPU v7x, 1024 devices: a whole 8x8x8 slice. The times are simulated.
1024 devices in a mesh: dp: 64 (over y_hi, z, core), ctx: 16 (over x, y_lo).
Axes of the slice: x: 8, y: 8 (y_hi: 4, y_lo: 2; y = y_hi * 2 + y_lo), z: 8, core: 2. Of those that a mesh axis runs over, the one named last changes fastest.
Arguments:
- qkv: bfloat16 [64, 2048, 5120], P('dp', 'ctx'), may hold values from -8 to 8
- dest: int32 [64, 32], P('dp'), may hold values from 0 to 63, as said below
- order: int32 [32], replicated, may hold values from 0 to 31, as said below
- lengths: int32 [64, 8], replicated, may hold values from 1 to 1024, 2048 in all within a row
Outputs:
- attended: bfloat16 [64, 2048, 4096], P('dp', 'ctx')
Inputs may be any that keep to these rules, and one draw needn't show every extreme that they name: `dest`: entry [r, s] is r itself, r + 1 or r - 1 (indices modulo 64), and the relation is mutual: if entry [r, s] is t, entry [t, s] is r. For every c below 16: order[2 c] is below 16 and order[2 c + 1] = 31 - order[2 c]; every span appears once.
All inputs are finite; a program needn't handle non-finite values.
Results may differ from a plain program's by a relative error of at most 0.0031.
Values may be sent and summed in bfloat16 or wider, within the bound.
No kernel may reach another device: no remote copies, remote signals or barrier semaphores. Data moves between devices by JAX's collectives and lax.ppermute only.
A program may use at most 64 MiB of HBM per device.

v0:
```python
import functools
import math

import jax
import jax.numpy as jnp
from jax import lax
from jax.experimental import pallas as pl
from jax.experimental.pallas import tpu as pltpu
from jax.sharding import Mesh
from jax.sharding import PartitionSpec as P


QUERY_HEADS = 32
KEY_VALUE_HEADS = 4
HEAD_SIZE = 128
NDOC = 8
SPAN = 64
QUERIES_PER_KV = 8
CTX = ("ctx_0", "ctx_1")
QUERY_WIDTH = QUERY_HEADS * HEAD_SIZE
HALF_WIDTH = KEY_VALUE_HEADS * HEAD_SIZE
SPANS = 32
CHUNK = 4
MOST_CHUNKS = 5
LISTED, BASES, WANTED = 0, 40, 80
ENDS, WHICH, POSITION, CHUNKS = 112, 120, 121, 122
PLAN = 128
KEEP = pl.ANY
FAR = 1 << 20
MASK_FLOOR = -1e30
EXP2_SCALE = math.log2(math.e) / math.sqrt(HEAD_SIZE)


def piece_slot(where_ref, piece):
    _, _, step, flip, part = piece
    column, row = where_ref[1], where_ref[2]
    there = (column + (1 - 2 * (column & 1)) * step) & 7
    return 2 * (2 * there + (row ^ flip)) + part


def list_kernel(pieces, where_ref, dest_ref, order_ref, lengths_ref, plan_ref):
    own_slot = 2 * (2 * where_ref[1] + where_ref[2])
    sources, spans, firsts = [], [], []
    for half in range(2):
        source = dest_ref[0, own_slot + half]
        plan_ref[half, WHICH] = jnp.where(
            source == where_ref[3], 1, jnp.where(source == where_ref[4], 2, 0)
        )
        span = order_ref[own_slot + half]
        plan_ref[half, POSITION] = span * SPAN
        end, first = jnp.int32(0), jnp.int32(0)
        for doc in range(NDOC):
            end = end + lengths_ref[source, doc]
            plan_ref[half, ENDS + doc] = end
            first = jnp.where(end <= span * SPAN, end, first)
        sources.append(source)
        spans.append(span)
        firsts.append(first)
    counts = [jnp.int32(0), jnp.int32(0)]
    for index, piece in enumerate(pieces):
        slot = piece_slot(where_ref, piece)
        source, span = dest_ref[0, slot], order_ref[slot]
        for half in range(2):
            need = (
                (source == sources[half])
                & (span <= spans[half])
                & (span * SPAN + SPAN > firsts[half])
            )
            plan_ref[half, LISTED + counts[half]] = index
            plan_ref[half, BASES + counts[half]] = span * SPAN
            need = need.astype(jnp.int32)
            plan_ref[half, WANTED + index] = need
            counts[half] = counts[half] + need
    for half in range(2):
        plan_ref[half, CHUNKS] = (counts[half] + CHUNK - 1) // CHUNK
        for extra in range(CHUNK - 1):
            plan_ref[half, LISTED + counts[half] + extra] = half
            plan_ref[half, BASES + counts[half] + extra] = FAR


def attention_kernel(pieces, count, *refs):
    plan = refs[0]
    query_refs = refs[1:4]
    piece_refs = refs[4 : 4 + count]
    out_ref = refs[4 + count]
    (queries, keys, values, scores, peaks, sums, mixed, outs, query_sems, piece_sems, out_sems) = refs[
        5 + count :
    ]

    def query_copy(half, which):
        rows = pl.ds(half * SPAN, SPAN)
        return pltpu.make_async_copy(
            query_refs[which].at[rows, pl.ds(0, QUERY_WIDTH)],
            queries.at[half],
            query_sems.at[half],
        )

    def out_copy(half):
        return pltpu.make_async_copy(
            outs.at[half], out_ref.at[pl.ds(half * SPAN, SPAN)], out_sems.at[half]
        )

    def piece_copies(index):
        ref, first_row = pieces[index][0], pieces[index][1]
        rows = pl.ds(first_row, SPAN)
        there = pl.ds(index * SPAN, SPAN)
        return (
            pltpu.make_async_copy(
                piece_refs[ref].at[rows, pl.ds(0, HALF_WIDTH)], keys.at[there], piece_sems.at[index, 0]
            ),
            pltpu.make_async_copy(
                piece_refs[ref].at[rows, pl.ds(HALF_WIDTH, HALF_WIDTH)],
                values.at[there],
                piece_sems.at[index, 1],
            ),
        )

    for half in range(2):
        for which in range(3):

            @pl.when(plan[half, WHICH] == which)
            def _(half=half, which=which):
                query_copy(half, which).start()

    for index in range(SPANS):

        @pl.when(plan[0, WANTED + index] + plan[1, WANTED + index] > 0)
        def _(index=index):
            for copy in piece_copies(index):
                copy.start()

    for half in range(2):
        query_copy(half, 0).wait()
    for index in range(SPANS):

        @pl.when(plan[0, WANTED + index] + plan[1, WANTED + index] > 0)
        def _(index=index):
            for copy in piece_copies(index):
                copy.wait()

    lane = lax.broadcasted_iota(jnp.int32, (1, CHUNK * SPAN), 1)
    rows = QUERIES_PER_KV * SPAN

    def one_half(half, unused):
        position = plan[half, POSITION] + lax.broadcasted_iota(jnp.int32, (SPAN, 1), 0)
        start = jnp.zeros((SPAN, 1), jnp.int32)
        for doc in range(NDOC):
            end = plan[half, ENDS + doc]
            start = jnp.where(position >= end, end, start)
        chunks = plan[half, CHUNKS]
        peaks[...] = jnp.full_like(peaks, MASK_FLOOR)
        sums[...] = jnp.zeros_like(sums)
        mixed[...] = jnp.zeros_like(mixed)

        def first_rows(chunk):
            return [
                pl.multiple_of(plan[half, LISTED + chunk * CHUNK + j] * SPAN, SPAN)
                for j in range(CHUNK)
            ]

        def score_chunk(chunk, carry):
            at = BASES + chunk * CHUNK
            base = jnp.full((1, CHUNK * SPAN), plan[half, at], jnp.int32)
            for j in range(1, CHUNK):
                base = jnp.where(lane >= j * SPAN, plan[half, at + j], base)
            key_position = (lane & (SPAN - 1)) + base
            visible = (key_position <= position) & (key_position >= start)
            bias = jnp.where(visible, 0.0, MASK_FLOOR).astype(jnp.float32)
            firsts_of = first_rows(chunk)
            for group in range(KEY_VALUE_HEADS):
                columns = slice(group * HEAD_SIZE, (group + 1) * HEAD_SIZE)
                key = jnp.concatenate([keys[pl.ds(f, SPAN), columns] for f in firsts_of], axis=0)
                query = jnp.concatenate(
                    [
                        queries[half, :, pl.ds((group * QUERIES_PER_KV + h) * HEAD_SIZE, HEAD_SIZE)]
                        for h in range(QUERIES_PER_KV)
                    ],
                    axis=0,
                )
                score = lax.dot_general(
                    query, key, (((1,), (1,)), ((), ())), preferred_element_type=jnp.float32
                )
                score = score.reshape(QUERIES_PER_KV, SPAN, CHUNK * SPAN) * EXP2_SCALE + bias[None]
                score = score.reshape(rows, CHUNK * SPAN)
                scores[chunk, group] = score
                peak = peaks[group]
                for j in range(0, CHUNK * SPAN, HEAD_SIZE):
                    peak = jnp.maximum(peak, score[:, j : j + HEAD_SIZE])
                peaks[group] = peak
            return carry

        lax.fori_loop(0, chunks, score_chunk, 0)
        for group in range(KEY_VALUE_HEADS):
            peaks[group] = jnp.broadcast_to(
                jnp.max(peaks[group], axis=1, keepdims=True), (rows, HEAD_SIZE)
            )

        def mix_chunk(chunk, carry):
            firsts_of = first_rows(chunk)
            for group in range(KEY_VALUE_HEADS):
                columns = slice(group * HEAD_SIZE, (group + 1) * HEAD_SIZE)
                value = jnp.concatenate([values[pl.ds(f, SPAN), columns] for f in firsts_of], axis=0)
                peak = peaks[group]
                total = sums[group]
                weights = []
                for j in range(0, CHUNK * SPAN, HEAD_SIZE):
                    weight = jnp.exp2(scores[chunk, group, :, j : j + HEAD_SIZE] - peak)
                    total = total + weight
                    weights.append(weight.astype(jnp.bfloat16))
                sums[group] = total
                mixed[group] += jnp.dot(
                    jnp.concatenate(weights, axis=1), value, preferred_element_type=jnp.float32
                )
            return carry

        lax.fori_loop(0, chunks, mix_chunk, 0)
        for group in range(KEY_VALUE_HEADS):
            total = jnp.sum(sums[group], axis=1, keepdims=True)
            result = (mixed[group] * (1.0 / total)).astype(jnp.bfloat16)
            for h in range(QUERIES_PER_KV):
                outs[half, :, pl.ds((group * QUERIES_PER_KV + h) * HEAD_SIZE, HEAD_SIZE)] = result[
                    h * SPAN : (h + 1) * SPAN
                ]
        out_copy(half).start()
        return unused

    lax.fori_loop(0, 2, one_half, 0)
    for half in range(2):
        out_copy(half).wait()


def list_key_spans(where, dest, order, lengths, pieces):
    smem = pl.BlockSpec(memory_space=pltpu.SMEM)
    return pl.pallas_call(
        functools.partial(list_kernel, pieces),
        out_shape=jax.ShapeDtypeStruct((2, PLAN), jnp.int32),
        in_specs=[smem] * 4,
        out_specs=smem,
        cost_estimate=pl.CostEstimate(flops=4_000_000, bytes_accessed=4_000, transcendentals=0),
        name="list_spans",
    )(where, dest, order, lengths)


def attention(plan, query_arrays, arrays, pieces):
    count = len(arrays)
    smem = pl.BlockSpec(memory_space=pltpu.SMEM)
    anywhere = pl.BlockSpec(memory_space=KEEP)
    rows = QUERIES_PER_KV * SPAN
    return pl.pallas_call(
        functools.partial(attention_kernel, pieces, count),
        out_shape=jax.ShapeDtypeStruct((2 * SPAN, QUERY_WIDTH), jnp.bfloat16),
        in_specs=[smem] + [anywhere] * (3 + count),
        out_specs=pl.BlockSpec(memory_space=KEEP),
        scratch_shapes=[
            pltpu.VMEM((2, SPAN, QUERY_WIDTH), jnp.bfloat16),
            pltpu.VMEM((SPANS * SPAN, HALF_WIDTH), jnp.bfloat16),
            pltpu.VMEM((SPANS * SPAN, HALF_WIDTH), jnp.bfloat16),
            pltpu.VMEM((MOST_CHUNKS, KEY_VALUE_HEADS, rows, CHUNK * SPAN), jnp.float32),
            pltpu.VMEM((KEY_VALUE_HEADS, rows, HEAD_SIZE), jnp.float32),
            pltpu.VMEM((KEY_VALUE_HEADS, rows, HEAD_SIZE), jnp.float32),
            pltpu.VMEM((KEY_VALUE_HEADS, rows, HEAD_SIZE), jnp.float32),
            pltpu.VMEM((2, SPAN, QUERY_WIDTH), jnp.bfloat16),
            pltpu.SemaphoreType.DMA((2,)),
            pltpu.SemaphoreType.DMA((SPANS, 2)),
            pltpu.SemaphoreType.DMA((2,)),
        ],
        cost_estimate=pl.CostEstimate(
            flops=1_000_000_000, bytes_accessed=4_000_000, transcendentals=2_000_000
        ),
        name="attend",
    )(plan, *query_arrays, *arrays)


def swaps(count, first):
    pairs = [(i % count, (i + 1) % count) for i in range(first, first + count, 2)]
    return pairs + [(b, a) for a, b in pairs]


def on_device(qkv, dest, order, lengths):
    dp_count = lax.axis_size("dp")
    dp_index = lax.axis_index("dp")
    column = lax.axis_index("ctx_0")
    row = lax.axis_index("ctx_1")
    columns = lax.axis_size("ctx_0")
    odd = dp_index & 1
    even_partner = dp_index + 1 - 2 * odd
    odd_partner = (dp_index - 1 + 2 * odd + dp_count) % dp_count
    resident = qkv[0]

    def trade(array, first):
        return lax.ppermute(array, "dp", swaps(dp_count, first))

    kv = resident[:, QUERY_WIDTH:]
    query_odd = trade(resident, 1)
    even_rows = trade(resident, 0)
    kv_odd = trade(kv, 1)
    kv_even = even_rows[:, QUERY_WIDTH:]
    own_sources = lax.dynamic_slice_in_dim(dest[0], 2 * (2 * column + row), 2)
    row_from = jnp.repeat(own_sources, SPAN)[:, None]
    own = jnp.where(
        row_from == even_partner, kv_even, jnp.where(row_from == odd_partner, kv_odd, kv)
    )
    other = lax.ppermute(own, "ctx_1", [(0, 1), (1, 0)])

    def across(array, first):
        return lax.ppermute(array, "ctx_0", swaps(columns, first))

    arrays = [own, other]
    ways = [0, 0]
    last = []
    for stream in (own, other):
        even, odd_side = stream, stream
        for step in range(1, 4):
            even, odd_side = across(odd_side, 0), across(even, 1)
            arrays += [even, odd_side]
            ways += [step, -step]
        last.append((even, odd_side))
    arrays += [across(last[0][1], 0), across(last[1][0], 1)]
    ways += [4, 4]
    flips = [0, 1] + [0] * 6 + [1] * 6 + [0, 1]
    pieces = [
        (index, part * SPAN, ways[index], flips[index], part)
        for index in range(len(arrays))
        for part in range(2)
    ]
    lane = jnp.arange(8, dtype=jnp.int32)
    where = jnp.where(
        lane == 0,
        dp_index,
        jnp.where(
            lane == 1,
            column,
            jnp.where(lane == 2, row, jnp.where(lane == 3, even_partner, odd_partner)),
        ),
    ).astype(jnp.int32)
    plan = list_key_spans(where, dest, order, lengths, pieces)
    attended = attention(plan, (resident, even_rows, query_odd), arrays, pieces)
    return attended[None]


def solution(mesh):
    finer = Mesh(mesh.devices.reshape(mesh.shape["dp"], 8, 2), ("dp", "ctx_0", "ctx_1"))
    placed = (P("dp", CTX, None), P("dp", None), P(), P())

    return jax.shard_map(
        on_device, mesh=finer, in_specs=placed, out_specs=P("dp", CTX, None), check_vma=False
    )
```

profile of v0, /device:TPU:22, one launch (start us, length us, event | category | flops | bytes accessed | tf_op | source)
XLA Modules:
  0.0 105.8 jit_solution(10359930315962735538)
XLA Ops:
  0.0 2.0 %collective-permute-start = (bf16[128,5120]{1,0:T(8,128)(2,1)}, bf16[128,5120]{1,0:T(8,128)(2,1)S(1)}, u32[]{:S(2)}, u32[]{:S(2)}) collective-permute-start(bf16[128,5120]{1,0:T(8,128)(2,1)} %bitcast.6), channel_id=1, source_target_pairs={{0,16},{32,48},{64,80},{96,112},{128,144},{160,176},{192,208},{224... | collective-permute-start | bytes 3932168 | tf_op jit(solution)/shard_map/ppermute | solution.py:291
  2.1 1.0 slice.9
  3.0 20.9 %collective-permute-start.2 = (bf16[128,1024]{1,0:T(8,128)(2,1)S(1)}, bf16[128,1024]{1,0:T(8,128)(2,1)S(1)}, u32[]{:S(2)}, u32[]{:S(2)}) collective-permute-start(bf16[128,1024]{1,0:T(8,128)(2,1)S(1)} %slice.9), channel_id=1, source_target_pairs={{16,32},{48,64},{80,96},{112,128},{144,160},{176,192},{208,224},{2... | collective-permute-start | bytes 786440 | tf_op jit(solution)/shard_map/ppermute | solution.py:291
  24.0 0.7 compare_bitcast_fusion.1
  24.7 0.1 broadcast_in_dim.44
  24.8 0.1 eq.57
  24.8 0.1 broadcast_in_dim.46
  24.9 0.1 eq.61
  25.0 5.8 %collective-permute-done.2 = bf16[128,1024]{1,0:T(8,128)(2,1)S(1)} collective-permute-done((bf16[128,1024]{1,0:T(8,128)(2,1)S(1)}, bf16[128,1024]{1,0:T(8,128)(2,1)S(1)}, u32[]{:S(2)}, u32[]{:S(2)}) %collective-permute-start.2) | collective-permute-done | bytes 262176 | tf_op jit(solution)/shard_map/ppermute | solution.py:291
  30.8 0.0 collective-permute-done.refs_2_
  30.8 1.2 %slice_select_fusion.refs_4_ = bf16[128,1024]{1,0:T(8,128)(2,1)S(1)} fusion(bf16[128,5120]{1,0:T(8,128)(2,1)S(1)} %collective-permute-done.refs_2_, bf16[128,1024]{1,0:T(8,128)(2,1)S(1)} %collective-permute-done.2, pred[128]{0:T(512)(128)(4,1)S(1)} %eq.61, pred[128]{0:T(512)(128)(4,1)S(1)} %eq.57, bf16[128,5120]{1,0:T(8,128)(2,1)} %bitcast.8), kind=kLoop, calls=%fused_computation | loop fusion | flops 262144 | bytes 1048832 | tf_op jit(solution)/shard_map/jit(_where)/select_n | solution.py:300
  32.0 3.0 %collective-permute-start.3 = (bf16[128,1024]{1,0:T(8,128)(2,1)S(1)}, bf16[128,1024]{1,0:T(8,128)(2,1)S(1)}, u32[]{:S(2)}, u32[]{:S(2)}) collective-permute-start(bf16[128,1024]{1,0:T(8,128)(2,1)S(1)} %slice_select_fusion.refs_4_), channel_id=1, source_target_pairs={{0,1},{1,0},{2,3},{3,2},{4,5},{5,4},{6,7},{7,6},{8,9},{9,8},{10,11... | collective-permute-start | bytes 786440 | tf_op jit(solution)/shard_map/ppermute | solution.py:303
  35.0 7.7 %collective-permute-start.1 = (bf16[128,5120]{1,0:T(8,128)(2,1)S(1)}, bf16[128,5120]{1,0:T(8,128)(2,1)}, u32[]{:S(2)}, u32[]{:S(2)}) collective-permute-start(bf16[128,5120]{1,0:T(8,128)(2,1)S(1)} %bitcast.10), channel_id=1, source_target_pairs={{16,32},{48,64},{80,96},{112,128},{144,160},{176,192},{208,224},{2... | collective-permute-start | bytes 3932168 | tf_op jit(solution)/shard_map/ppermute | solution.py:291
  42.8 4.6 %collective-permute-start.5 = (bf16[128,1024]{1,0:T(8,128)(2,1)S(1)}, bf16[128,1024]{1,0:T(8,128)(2,1)S(1)}, u32[]{:S(2)}, u32[]{:S(2)}) collective-permute-start(bf16[128,1024]{1,0:T(8,128)(2,1)S(1)} %slice_select_fusion.refs_4_), channel_id=1, source_target_pairs={{2,4},{6,8},{10,12},{14,0},{4,2},{8,6},{12,10},{0,14},{3,5},{7,9},... | collective-permute-start | bytes 786440 | tf_op jit(solution)/shard_map/ppermute | solution.py:306
  47.4 0.0 collective-permute-done.3.refs_5_
  47.4 1.9 %collective-permute-start.10 = (bf16[128,1024]{1,0:T(8,128)(2,1)S(1)}, bf16[128,1024]{1,0:T(8,128)(2,1)S(1)}, u32[]{:S(2)}, u32[]{:S(2)}) collective-permute-start(bf16[128,1024]{1,0:T(8,128)(2,1)S(1)} %collective-permute-done.3.refs_5_), channel_id=1, source_target_pairs={{0,2},{4,6},{8,10},{12,14},{2,0},{6,4},{10,8},{14,12},{1,3},{5,7},... | collective-permute-start | bytes 786440 | tf_op jit(solution)/shard_map/ppermute | solution.py:306
  49.3 3.9 %collective-permute-start.4 = (bf16[128,1024]{1,0:T(8,128)(2,1)S(1)}, bf16[128,1024]{1,0:T(8,128)(2,1)S(1)}, u32[]{:S(2)}, u32[]{:S(2)}) collective-permute-start(bf16[128,1024]{1,0:T(8,128)(2,1)S(1)} %slice_select_fusion.refs_4_), channel_id=1, source_target_pairs={{0,2},{4,6},{8,10},{12,14},{2,0},{6,4},{10,8},{14,12},{1,3},{5,7},... | collective-permute-start | bytes 786440 | tf_op jit(solution)/shard_map/ppermute | solution.py:306
  53.3 0.0 collective-permute-done.5.refs_7_
  53.3 3.0 %collective-permute-start.6 = (bf16[128,1024]{1,0:T(8,128)(2,1)S(1)}, bf16[128,1024]{1,0:T(8,128)(2,1)S(1)}, u32[]{:S(2)}, u32[]{:S(2)}) collective-permute-start(bf16[128,1024]{1,0:T(8,128)(2,1)S(1)} %collective-permute-done.5.refs_7_), channel_id=1, source_target_pairs={{0,2},{4,6},{8,10},{12,14},{2,0},{6,4},{10,8},{14,12},{1,3},{5,7},... | collective-permute-start | bytes 786440 | tf_op jit(solution)/shard_map/ppermute | solution.py:306
  56.3 4.7 %collective-permute-start.11 = (bf16[128,1024]{1,0:T(8,128)(2,1)S(1)}, bf16[128,1024]{1,0:T(8,128)(2,1)S(1)}, u32[]{:S(2)}, u32[]{:S(2)}) collective-permute-start(bf16[128,1024]{1,0:T(8,128)(2,1)S(1)} %collective-permute-done.3.refs_5_), channel_id=1, source_target_pairs={{2,4},{6,8},{10,12},{14,0},{4,2},{8,6},{12,10},{0,14},{3,5},{7,9},... | collective-permute-start | bytes 786440 | tf_op jit(solution)/shard_map/ppermute | solution.py:306
  61.0 0.0 collective-permute-done.10.refs_12_
  61.0 2.4 %collective-permute-start.13 = (bf16[128,1024]{1,0:T(8,128)(2,1)S(1)}, bf16[128,1024]{1,0:T(8,128)(2,1)S(1)}, u32[]{:S(2)}, u32[]{:S(2)}) collective-permute-start(bf16[128,1024]{1,0:T(8,128)(2,1)S(1)} %collective-permute-done.10.refs_12_), channel_id=1, source_target_pairs={{2,4},{6,8},{10,12},{14,0},{4,2},{8,6},{12,10},{0,14},{3,5},{7,9},... | collective-permute-start | bytes 786440 | tf_op jit(solution)/shard_map/ppermute | solution.py:306
  63.4 0.7 collective-permute-done.4.refs_6_
  64.1 4.0 %collective-permute-start.7 = (bf16[128,1024]{1,0:T(8,128)(2,1)S(1)}, bf16[128,1024]{1,0:T(8,128)(2,1)}, u32[]{:S(2)}, u32[]{:S(2)}) collective-permute-start(bf16[128,1024]{1,0:T(8,128)(2,1)S(1)} %collective-permute-done.4.refs_6_), channel_id=1, source_target_pairs={{2,4},{6,8},{10,12},{14,0},{4,2},{8,6},{12,10},{0,14},{3,5},{7,9},... | collective-permute-start | bytes 786440 | tf_op jit(solution)/shard_map/ppermute | solution.py:306
  68.1 1.6 %collective-permute-done.6.refs_8_ = bf16[128,1024]{1,0:T(8,128)(2,1)S(1)} collective-permute-done((bf16[128,1024]{1,0:T(8,128)(2,1)S(1)}, bf16[128,1024]{1,0:T(8,128)(2,1)S(1)}, u32[]{:S(2)}, u32[]{:S(2)}) %collective-permute-start.6) | collective-permute-done | bytes 262176 | tf_op jit(solution)/shard_map/ppermute | solution.py:306
  69.7 1.9 %collective-permute-start.9 = (bf16[128,1024]{1,0:T(8,128)(2,1)S(1)}, bf16[128,1024]{1,0:T(8,128)(2,1)}, u32[]{:S(2)}, u32[]{:S(2)}) collective-permute-start(bf16[128,1024]{1,0:T(8,128)(2,1)S(1)} %collective-permute-done.6.refs_8_), channel_id=1, source_target_pairs={{2,4},{6,8},{10,12},{14,0},{4,2},{8,6},{12,10},{0,14},{3,5},{7,9},... | collective-permute-start | bytes 786440 | tf_op jit(solution)/shard_map/ppermute | solution.py:306
  71.6 0.0 collective-permute-done.11.refs_13_
  71.7 0.0 copy-done.5
  71.7 1.9 %collective-permute-start.12 = (bf16[128,1024]{1,0:T(8,128)(2,1)S(1)}, bf16[128,1024]{1,0:T(8,128)(2,1)}, u32[]{:S(2)}, u32[]{:S(2)}) collective-permute-start(bf16[128,1024]{1,0:T(8,128)(2,1)S(1)} %collective-permute-done.11.refs_13_), channel_id=1, source_target_pairs={{0,2},{4,6},{8,10},{12,14},{2,0},{6,4},{10,8},{14,12},{1,3},{5,7},... | collective-permute-start | bytes 786440 | tf_op jit(solution)/shard_map/ppermute | solution.py:306
  73.6 0.0 collective-permute-done.13.refs_15_
  73.6 3.9 %collective-permute-start.14 = (bf16[128,1024]{1,0:T(8,128)(2,1)S(1)}, bf16[128,1024]{1,0:T(8,128)(2,1)}, u32[]{:S(2)}, u32[]{:S(2)}) collective-permute-start(bf16[128,1024]{1,0:T(8,128)(2,1)S(1)} %collective-permute-done.13.refs_15_), channel_id=1, source_target_pairs={{0,2},{4,6},{8,10},{12,14},{2,0},{6,4},{10,8},{14,12},{1,3},{5,7},... | collective-permute-start | bytes 786440 | tf_op jit(solution)/shard_map/ppermute | solution.py:306
  77.6 0.0 collective-permute-done.7.refs_9_
  77.6 1.9 %collective-permute-start.8 = (bf16[128,1024]{1,0:T(8,128)(2,1)}, bf16[128,1024]{1,0:T(8,128)(2,1)}, u32[]{:S(2)}, u32[]{:S(2)}) collective-permute-start(bf16[128,1024]{1,0:T(8,128)(2,1)} %collective-permute-done.7.refs_9_), channel_id=1, source_target_pairs={{0,2},{4,6},{8,10},{12,14},{2,0},{6,4},{10,8},{14,12},{1,3},{5,7},... | collective-permute-start | bytes 786440 | tf_op jit(solution)/shard_map/ppermute | solution.py:306
  79.5 0.6 collective-permute-done.9.refs_11_
  80.2 3.3 %collective-permute-start.16 = (bf16[128,1024]{1,0:T(8,128)(2,1)}, bf16[128,1024]{1,0:T(8,128)(2,1)}, u32[]{:S(2)}, u32[]{:S(2)}) collective-permute-start(bf16[128,1024]{1,0:T(8,128)(2,1)} %collective-permute-done.9.refs_11_), channel_id=1, source_target_pairs={{0,2},{4,6},{8,10},{12,14},{2,0},{6,4},{10,8},{14,12},{1,3},{5,7},... | collective-permute-start | bytes 786440 | tf_op jit(solution)/shard_map/ppermute | solution.py:306
  83.5 0.0 collective-permute-done.12.refs_14_
  83.5 5.1 %collective-permute-start.15 = (bf16[128,1024]{1,0:T(8,128)(2,1)}, bf16[128,1024]{1,0:T(8,128)(2,1)}, u32[]{:S(2)}, u32[]{:S(2)}) collective-permute-start(bf16[128,1024]{1,0:T(8,128)(2,1)} %collective-permute-done.12.refs_14_), channel_id=1, source_target_pairs={{2,4},{6,8},{10,12},{14,0},{4,2},{8,6},{12,10},{0,14},{3,5},{7,9},... | collective-permute-start | bytes 786440 | tf_op jit(solution)/shard_map/ppermute | solution.py:306
  88.6 0.0 collective-permute-done.14.refs_16_
  88.6 1.9 %collective-permute-start.17 = (bf16[128,1024]{1,0:T(8,128)(2,1)}, bf16[128,1024]{1,0:T(8,128)(2,1)}, u32[]{:S(2)}, u32[]{:S(2)}) collective-permute-start(bf16[128,1024]{1,0:T(8,128)(2,1)} %collective-permute-done.14.refs_16_), channel_id=1, source_target_pairs={{2,4},{6,8},{10,12},{14,0},{4,2},{8,6},{12,10},{0,14},{3,5},{7,9},... | collective-permute-start | bytes 786440 | tf_op jit(solution)/shard_map/ppermute | solution.py:306
  90.6 0.7 copy.5.lengths_ref
  91.3 0.5 compare_select_fusion.3.where_ref
  91.8 2.2 %list_spans.1.refs_0_ = s32[2,128]{1,0:T(2,128)} custom-call(s32[8]{0:T(128)} %compare_select_fusion.3.where_ref, s32[1,32]{1,0:T(1,128)} %dest_ref.1, s32[32]{0:T(128)} %order_ref.1, s32[64,8]{1,0:T(8,128)} %copy.5.lengths_ref), custom_call_target="tpu_custom_call" | custom-call | flops 4000000 | bytes 4000 | tf_op jit(solution)/shard_map/list_spans/pallas_call | solution.py:234
  94.0 0.0 collective-permute-done.1.refs_3_
  94.0 0.0 collective-permute-done.8.refs_10_
  94.0 0.0 collective-permute-done.16.refs_18_
  94.1 0.0 collective-permute-done.15.refs_17_
  94.1 4.4 %collective-permute-done.17.refs_19_ = bf16[128,1024]{1,0:T(8,128)(2,1)} collective-permute-done((bf16[128,1024]{1,0:T(8,128)(2,1)}, bf16[128,1024]{1,0:T(8,128)(2,1)}, u32[]{:S(2)}, u32[]{:S(2)}) %collective-permute-start.17) | collective-permute-done | bytes 262176 | tf_op jit(solution)/shard_map/ppermute | solution.py:306
  98.5 7.3 %attend.1 = bf16[128,4096]{1,0:T(8,128)(2,1)} custom-call(s32[2,128]{1,0:T(2,128)} %list_spans.1.refs_0_, bf16[128,5120]{1,0:T(8,128)(2,1)} %bitcast.9, bf16[128,5120]{1,0:T(8,128)(2,1)} %copy-done.1, bf16[128,5120]{1,0:T(8,128)(2,1)} %collective-permute-done.1.refs_3_, bf16[128,1024]{1,0:T(8,128)(2,1)} %copy-done.2, bf16[128,1024]{1,0:T(8,128)(2,1)} %copy-done.3, ...), custom_call_target="tpu_custom_call" | custom-call | flops 1000000000 | bytes 4000000 | tf_op jit(solution)/shard_map/attend/pallas_call | solution.py:249
  (21 shorter events, 0.0 us)
Async XLA Ops:
  0.0 35.0 %copy-start = (bf16[1,128,5120]{2,1,0:T(8,128)(2,1)S(1)}, bf16[1,128,5120]{2,1,0:T(8,128)(2,1)}, u32[]{:S(2)}) copy-start(bf16[1,128,5120]{2,1,0:T(8,128)(2,1)} %param.4) | copy-start | bytes 3932164
  0.0 90.6 %copy-start.10 = (s32[64,8]{0,1:T(8,128)S(1)}, s32[64,8]{0,1:T(8,128)}, u32[]{:S(2)}) copy-start(s32[64,8]{0,1:T(8,128)} %param.7) | copy-start | bytes 6148
  0.0 30.8 %collective-permute-start = (bf16[128,5120]{1,0:T(8,128)(2,1)}, bf16[128,5120]{1,0:T(8,128)(2,1)S(1)}, u32[]{:S(2)}, u32[]{:S(2)}) collective-permute-start(bf16[128,5120]{1,0:T(8,128)(2,1)} %bitcast.6), channel_id=1, source_target_pairs={{0,16},{32,48},{64,80},{96,112},{128,144},{160,176},{192,208},{224... | collective-permute-start | bytes 3932168 | tf_op jit(solution)/shard_map/ppermute | solution.py:291
  3.0 27.7 %collective-permute-start.2 = (bf16[128,1024]{1,0:T(8,128)(2,1)S(1)}, bf16[128,1024]{1,0:T(8,128)(2,1)S(1)}, u32[]{:S(2)}, u32[]{:S(2)}) collective-permute-start(bf16[128,1024]{1,0:T(8,128)(2,1)S(1)} %slice.9), channel_id=1, source_target_pairs={{16,32},{48,64},{80,96},{112,128},{144,160},{176,192},{208,224},{2... | collective-permute-start | bytes 786440 | tf_op jit(solution)/shard_map/ppermute | solution.py:291
  30.8 67.7 %copy-start.1 = (bf16[128,5120]{1,0:T(8,128)(2,1)}, bf16[128,5120]{1,0:T(8,128)(2,1)S(1)}, u32[]{:S(2)}) copy-start(bf16[128,5120]{1,0:T(8,128)(2,1)S(1)} %collective-permute-done.refs_2_) | copy-start | bytes 3932164
  32.0 66.4 %copy-start.2 = (bf16[128,1024]{1,0:T(8,128)(2,1)}, bf16[128,1024]{1,0:T(8,128)(2,1)S(1)}, u32[]{:S(2)}) copy-start(bf16[128,1024]{1,0:T(8,128)(2,1)S(1)} %slice_select_fusion.refs_4_) | copy-start | bytes 786436
  32.0 15.4 %collective-permute-start.3 = (bf16[128,1024]{1,0:T(8,128)(2,1)S(1)}, bf16[128,1024]{1,0:T(8,128)(2,1)S(1)}, u32[]{:S(2)}, u32[]{:S(2)}) collective-permute-start(bf16[128,1024]{1,0:T(8,128)(2,1)S(1)} %slice_select_fusion.refs_4_), channel_id=1, source_target_pairs={{0,1},{1,0},{2,3},{3,2},{4,5},{5,4},{6,7},{7,6},{8,9},{9,8},{10,11... | collective-permute-start | bytes 786440 | tf_op jit(solution)/shard_map/ppermute | solution.py:303
  35.0 59.0 %collective-permute-start.1 = (bf16[128,5120]{1,0:T(8,128)(2,1)S(1)}, bf16[128,5120]{1,0:T(8,128)(2,1)}, u32[]{:S(2)}, u32[]{:S(2)}) collective-permute-start(bf16[128,5120]{1,0:T(8,128)(2,1)S(1)} %bitcast.10), channel_id=1, source_target_pairs={{16,32},{48,64},{80,96},{112,128},{144,160},{176,192},{208,224},{2... | collective-permute-start | bytes 3932168 | tf_op jit(solution)/shard_map/ppermute | solution.py:291
  42.8 10.5 %collective-permute-start.5 = (bf16[128,1024]{1,0:T(8,128)(2,1)S(1)}, bf16[128,1024]{1,0:T(8,128)(2,1)S(1)}, u32[]{:S(2)}, u32[]{:S(2)}) collective-permute-start(bf16[128,1024]{1,0:T(8,128)(2,1)S(1)} %slice_select_fusion.refs_4_), channel_id=1, source_target_pairs={{2,4},{6,8},{10,12},{14,0},{4,2},{8,6},{12,10},{0,14},{3,5},{7,9},... | collective-permute-start | bytes 786440 | tf_op jit(solution)/shard_map/ppermute | solution.py:306
  47.4 51.0 %copy-start.3 = (bf16[128,1024]{1,0:T(8,128)(2,1)}, bf16[128,1024]{1,0:T(8,128)(2,1)S(1)}, u32[]{:S(2)}) copy-start(bf16[128,1024]{1,0:T(8,128)(2,1)S(1)} %collective-permute-done.3.refs_5_) | copy-start | bytes 786436
  47.4 13.6 %collective-permute-start.10 = (bf16[128,1024]{1,0:T(8,128)(2,1)S(1)}, bf16[128,1024]{1,0:T(8,128)(2,1)S(1)}, u32[]{:S(2)}, u32[]{:S(2)}) collective-permute-start(bf16[128,1024]{1,0:T(8,128)(2,1)S(1)} %collective-permute-done.3.refs_5_), channel_id=1, source_target_pairs={{0,2},{4,6},{8,10},{12,14},{2,0},{6,4},{10,8},{14,12},{1,3},{5,7},... | collective-permute-start | bytes 786440 | tf_op jit(solution)/shard_map/ppermute | solution.py:306
  49.3 14.8 %collective-permute-start.4 = (bf16[128,1024]{1,0:T(8,128)(2,1)S(1)}, bf16[128,1024]{1,0:T(8,128)(2,1)S(1)}, u32[]{:S(2)}, u32[]{:S(2)}) collective-permute-start(bf16[128,1024]{1,0:T(8,128)(2,1)S(1)} %slice_select_fusion.refs_4_), channel_id=1, source_target_pairs={{0,2},{4,6},{8,10},{12,14},{2,0},{6,4},{10,8},{14,12},{1,3},{5,7},... | collective-permute-start | bytes 786440 | tf_op jit(solution)/shard_map/ppermute | solution.py:306
  53.3 45.2 %copy-start.4 = (bf16[128,1024]{1,0:T(8,128)(2,1)}, bf16[128,1024]{1,0:T(8,128)(2,1)S(1)}, u32[]{:S(2)}) copy-start(bf16[128,1024]{1,0:T(8,128)(2,1)S(1)} %collective-permute-done.5.refs_7_) | copy-start | bytes 786436
  53.3 16.4 %collective-permute-start.6 = (bf16[128,1024]{1,0:T(8,128)(2,1)S(1)}, bf16[128,1024]{1,0:T(8,128)(2,1)S(1)}, u32[]{:S(2)}, u32[]{:S(2)}) collective-permute-start(bf16[128,1024]{1,0:T(8,128)(2,1)S(1)} %collective-permute-done.5.refs_7_), channel_id=1, source_target_pairs={{0,2},{4,6},{8,10},{12,14},{2,0},{6,4},{10,8},{14,12},{1,3},{5,7},... | collective-permute-start | bytes 786440 | tf_op jit(solution)/shard_map/ppermute | solution.py:306
  56.3 15.4 %collective-permute-start.11 = (bf16[128,1024]{1,0:T(8,128)(2,1)S(1)}, bf16[128,1024]{1,0:T(8,128)(2,1)S(1)}, u32[]{:S(2)}, u32[]{:S(2)}) collective-permute-start(bf16[128,1024]{1,0:T(8,128)(2,1)S(1)} %collective-permute-done.3.refs_5_), channel_id=1, source_target_pairs={{2,4},{6,8},{10,12},{14,0},{4,2},{8,6},{12,10},{0,14},{3,5},{7,9},... | collective-permute-start | bytes 786440 | tf_op jit(solution)/shard_map/ppermute | solution.py:306
  61.0 10.7 %copy-start.5 = (bf16[128,1024]{1,0:T(8,128)(2,1)}, bf16[128,1024]{1,0:T(8,128)(2,1)S(1)}, u32[]{:S(2)}) copy-start(bf16[128,1024]{1,0:T(8,128)(2,1)S(1)} %collective-permute-done.10.refs_12_) | copy-start | bytes 786436
  61.0 12.6 %collective-permute-start.13 = (bf16[128,1024]{1,0:T(8,128)(2,1)S(1)}, bf16[128,1024]{1,0:T(8,128)(2,1)S(1)}, u32[]{:S(2)}, u32[]{:S(2)}) collective-permute-start(bf16[128,1024]{1,0:T(8,128)(2,1)S(1)} %collective-permute-done.10.refs_12_), channel_id=1, source_target_pairs={{2,4},{6,8},{10,12},{14,0},{4,2},{8,6},{12,10},{0,14},{3,5},{7,9},... | collective-permute-start | bytes 786440 | tf_op jit(solution)/shard_map/ppermute | solution.py:306
  64.1 9.5 %copy-start.6 = (bf16[128,1024]{1,0:T(8,128)(2,1)}, bf16[128,1024]{1,0:T(8,128)(2,1)S(1)}, u32[]{:S(2)}) copy-start(bf16[128,1024]{1,0:T(8,128)(2,1)S(1)} %collective-permute-done.4.refs_6_) | copy-start | bytes 786436
  64.1 13.5 %collective-permute-start.7 = (bf16[128,1024]{1,0:T(8,128)(2,1)S(1)}, bf16[128,1024]{1,0:T(8,128)(2,1)}, u32[]{:S(2)}, u32[]{:S(2)}) collective-permute-start(bf16[128,1024]{1,0:T(8,128)(2,1)S(1)} %collective-permute-done.4.refs_6_), channel_id=1, source_target_pairs={{2,4},{6,8},{10,12},{14,0},{4,2},{8,6},{12,10},{0,14},{3,5},{7,9},... | collective-permute-start | bytes 786440 | tf_op jit(solution)/shard_map/ppermute | solution.py:306
  69.7 7.9 %copy-start.7 = (bf16[128,1024]{1,0:T(8,128)(2,1)}, bf16[128,1024]{1,0:T(8,128)(2,1)S(1)}, u32[]{:S(2)}) copy-start(bf16[128,1024]{1,0:T(8,128)(2,1)S(1)} %collective-permute-done.6.refs_8_) | copy-start | bytes 786436
  69.7 10.4 %collective-permute-start.9 = (bf16[128,1024]{1,0:T(8,128)(2,1)S(1)}, bf16[128,1024]{1,0:T(8,128)(2,1)}, u32[]{:S(2)}, u32[]{:S(2)}) collective-permute-start(bf16[128,1024]{1,0:T(8,128)(2,1)S(1)} %collective-permute-done.6.refs_8_), channel_id=1, source_target_pairs={{2,4},{6,8},{10,12},{14,0},{4,2},{8,6},{12,10},{0,14},{3,5},{7,9},... | collective-permute-start | bytes 786440 | tf_op jit(solution)/shard_map/ppermute | solution.py:306
  71.7 8.5 %copy-start.8 = (bf16[128,1024]{1,0:T(8,128)(2,1)}, bf16[128,1024]{1,0:T(8,128)(2,1)S(1)}, u32[]{:S(2)}) copy-start(bf16[128,1024]{1,0:T(8,128)(2,1)S(1)} %collective-permute-done.11.refs_13_) | copy-start | bytes 786436
  71.7 11.8 %collective-permute-start.12 = (bf16[128,1024]{1,0:T(8,128)(2,1)S(1)}, bf16[128,1024]{1,0:T(8,128)(2,1)}, u32[]{:S(2)}, u32[]{:S(2)}) collective-permute-start(bf16[128,1024]{1,0:T(8,128)(2,1)S(1)} %collective-permute-done.11.refs_13_), channel_id=1, source_target_pairs={{0,2},{4,6},{8,10},{12,14},{2,0},{6,4},{10,8},{14,12},{1,3},{5,7},... | collective-permute-start | bytes 786440 | tf_op jit(solution)/shard_map/ppermute | solution.py:306
  73.6 9.9 %copy-start.9 = (bf16[128,1024]{1,0:T(8,128)(2,1)}, bf16[128,1024]{1,0:T(8,128)(2,1)S(1)}, u32[]{:S(2)}) copy-start(bf16[128,1024]{1,0:T(8,128)(2,1)S(1)} %collective-permute-done.13.refs_15_) | copy-start | bytes 786436
  73.6 15.0 %collective-permute-start.14 = (bf16[128,1024]{1,0:T(8,128)(2,1)S(1)}, bf16[128,1024]{1,0:T(8,128)(2,1)}, u32[]{:S(2)}, u32[]{:S(2)}) collective-permute-start(bf16[128,1024]{1,0:T(8,128)(2,1)S(1)} %collective-permute-done.13.refs_15_), channel_id=1, source_target_pairs={{0,2},{4,6},{8,10},{12,14},{2,0},{6,4},{10,8},{14,12},{1,3},{5,7},... | collective-permute-start | bytes 786440 | tf_op jit(solution)/shard_map/ppermute | solution.py:306
  77.6 16.4 %collective-permute-start.8 = (bf16[128,1024]{1,0:T(8,128)(2,1)}, bf16[128,1024]{1,0:T(8,128)(2,1)}, u32[]{:S(2)}, u32[]{:S(2)}) collective-permute-start(bf16[128,1024]{1,0:T(8,128)(2,1)} %collective-permute-done.7.refs_9_), channel_id=1, source_target_pairs={{0,2},{4,6},{8,10},{12,14},{2,0},{6,4},{10,8},{14,12},{1,3},{5,7},... | collective-permute-start | bytes 786440 | tf_op jit(solution)/shard_map/ppermute | solution.py:306
  80.2 13.9 %collective-permute-start.16 = (bf16[128,1024]{1,0:T(8,128)(2,1)}, bf16[128,1024]{1,0:T(8,128)(2,1)}, u32[]{:S(2)}, u32[]{:S(2)}) collective-permute-start(bf16[128,1024]{1,0:T(8,128)(2,1)} %collective-permute-done.9.refs_11_), channel_id=1, source_target_pairs={{0,2},{4,6},{8,10},{12,14},{2,0},{6,4},{10,8},{14,12},{1,3},{5,7},... | collective-permute-start | bytes 786440 | tf_op jit(solution)/shard_map/ppermute | solution.py:306
  83.5 10.6 %collective-permute-start.15 = (bf16[128,1024]{1,0:T(8,128)(2,1)}, bf16[128,1024]{1,0:T(8,128)(2,1)}, u32[]{:S(2)}, u32[]{:S(2)}) collective-permute-start(bf16[128,1024]{1,0:T(8,128)(2,1)} %collective-permute-done.12.refs_14_), channel_id=1, source_target_pairs={{2,4},{6,8},{10,12},{14,0},{4,2},{8,6},{12,10},{0,14},{3,5},{7,9},... | collective-permute-start | bytes 786440 | tf_op jit(solution)/shard_map/ppermute | solution.py:306
  88.6 9.8 %collective-permute-start.17 = (bf16[128,1024]{1,0:T(8,128)(2,1)}, bf16[128,1024]{1,0:T(8,128)(2,1)}, u32[]{:S(2)}, u32[]{:S(2)}) collective-permute-start(bf16[128,1024]{1,0:T(8,128)(2,1)} %collective-permute-done.14.refs_16_), channel_id=1, source_target_pairs={{2,4},{6,8},{10,12},{14,0},{4,2},{8,6},{12,10},{0,14},{3,5},{7,9},... | collective-permute-start | bytes 786440 | tf_op jit(solution)/shard_map/ppermute | solution.py:306
where the time goes:
time: 107 us; the launch traced here: 106 us
  starting transfers between devices  78.1 us (73%)
  waiting for transfers between devices  13.2 us (12%)
  Pallas kernels  9.56 us (9%)
  other arithmetic  2.44 us (2%)
  local copies, waits for them, and re-layouts  2.04 us (2%)
    ppermute x14, starting transfers between devices, across(): return lax.ppermute(array, 'ctx_0', swaps(columns, first))  44.5 us
    ppermute x3, starting transfers between devices, trade(): return lax.ppermute(array, 'dp', swaps(dp_count, first))  30.7 us
    ppermute x14, waiting for transfers between devices, across(): return lax.ppermute(array, 'ctx_0', swaps(columns, first))  7.42 us
    pallas_call x1, Pallas kernels, attention(): pl.pallas_call(functools.partial(attention_kernel, pieces, count), out_sh...  7.31 us
    ppermute x3, waiting for transfers between devices, trade(): return lax.ppermute(array, 'dp', swaps(dp_count, first))  5.77 us
    ppermute x1, starting transfers between devices, on_device(): other = lax.ppermute(own, 'ctx_1', [(0, 1), (1, 0)])  3 us
    pallas_call x1, Pallas kernels, list_key_spans(): pl.pallas_call(functools.partial(list_kernel, pieces), out_shape=jax.Shap...  2.25 us
  transfers between devices with their start and end apart: 18, of which 5 were waited for; matrix products, arithmetic and copies ran while one was open for 3% of the time, Pallas kernels for 2%

commit v1 on v0

--- a/solution.py
+++ b/solution.py
@@ -291,16 +291,22 @@
         return lax.ppermute(array, "dp", swaps(dp_count, first))
 
     kv = resident[:, QUERY_WIDTH:]
+    kv_across = lax.ppermute(kv, "ctx_1", [(0, 1), (1, 0)])
     query_odd = trade(resident, 1)
+    other_even = trade(kv_across, 0)
     even_rows = trade(resident, 0)
+    other_odd = trade(kv_across, 1)
     kv_odd = trade(kv, 1)
-    kv_even = even_rows[:, QUERY_WIDTH:]
-    own_sources = lax.dynamic_slice_in_dim(dest[0], 2 * (2 * column + row), 2)
-    row_from = jnp.repeat(own_sources, SPAN)[:, None]
-    own = jnp.where(
-        row_from == even_partner, kv_even, jnp.where(row_from == odd_partner, kv_odd, kv)
-    )
-    other = lax.ppermute(own, "ctx_1", [(0, 1), (1, 0)])
+
+    def settled(at_row, kept, from_even, from_odd):
+        sources = lax.dynamic_slice_in_dim(dest[0], 2 * (2 * column + at_row), 2)
+        row_from = jnp.repeat(sources, SPAN)[:, None]
+        return jnp.where(
+            row_from == even_partner, from_even, jnp.where(row_from == odd_partner, from_odd, kept)
+        )
+
+    own = settled(row, kv, even_rows[:, QUERY_WIDTH:], kv_odd)
+    other = settled(1 - row, kv_across, other_even, other_odd)
 
     def across(array, first):
         return lax.ppermute(array, "ctx_0", swaps(columns, first))

time: 107 us -> 117 us (1.093)
  the two profiles are of different devices: /device:TPU:22 before, /device:TPU:20 now
where the time goes in v1:
time: 117 us; the launch traced here: 116 us
  starting transfers between devices  82.1 us (70%)
  waiting for transfers between devices  15.7 us (13%)
  Pallas kernels  10.6 us (9%)
  local copies, waits for them, and re-layouts  3.77 us (3%)
  other arithmetic  3.76 us (3%)
    ppermute x14, starting transfers between devices, across(): return lax.ppermute(array, 'ctx_0', swaps(columns, first))  46.2 us
    ppermute x5, starting transfers between devices, trade(): return lax.ppermute(array, 'dp', swaps(dp_count, first))  33.7 us
    ppermute x1, waiting for transfers between devices, on_device(): kv_across = lax.ppermute(kv, 'ctx_1', [(0, 1), (1, 0)])  8.65 us
    pallas_call x1, Pallas kernels, attention(): pl.pallas_call(functools.partial(attention_kernel, pieces, count), out_sh...  8.36 us
    ppermute x5, waiting for transfers between devices, trade(): return lax.ppermute(array, 'dp', swaps(dp_count, first))  3.93 us
    ppermute x14, waiting for transfers between devices, across(): return lax.ppermute(array, 'ctx_0', swaps(columns, first))  3.08 us
    select_n x2, other arithmetic, settled(): jnp.where(row_from == even_partner, from_even, jnp.where(row_from == odd_...  2.36 us
  transfers between devices with their start and end apart: 20, of which 3 were waited for; matrix products, arithmetic and copies ran while one was open for 6% of the time, Pallas kernels for 2%

profile of v1, /device:TPU:20, one launch (start us, length us, event | category | flops | bytes accessed | tf_op | source)
XLA Modules:
  0.0 116.4 jit_solution(7100042075547221129)
XLA Ops:
  0.0 2.0 %collective-permute-start = (bf16[128,5120]{1,0:T(8,128)(2,1)}, bf16[128,5120]{1,0:T(8,128)(2,1)S(1)}, u32[]{:S(2)}, u32[]{:S(2)}) collective-permute-start(bf16[128,5120]{1,0:T(8,128)(2,1)} %bitcast.10), channel_id=1, source_target_pairs={{0,16},{32,48},{64,80},{96,112},{128,144},{160,176},{192,208},{224... | collective-permute-start | bytes 3932168 | tf_op jit(solution)/shard_map/ppermute | solution.py:291
  2.1 1.7 %slice.9 = bf16[128,1024]{1,0:T(8,128)(2,1)} slice(bf16[128,5120]{1,0:T(8,128)(2,1)} %bitcast.11), slice={[0:128], [4096:5120]} | slice | bytes 524288 | tf_op jit(solution)/shard_map/slice | solution.py:293
  3.7 2.2 %collective-permute-start.3 = (bf16[128,1024]{1,0:T(8,128)(2,1)}, bf16[128,1024]{1,0:T(8,128)(2,1)S(1)}, u32[]{:S(2)}, u32[]{:S(2)}) collective-permute-start(bf16[128,1024]{1,0:T(8,128)(2,1)} %slice.9), channel_id=1, source_target_pairs={{0,1},{1,0},{2,3},{3,2},{4,5},{5,4},{6,7},{7,6},{8,9},{9,8},{10,11... | collective-permute-start | bytes 786440 | tf_op jit(solution)/shard_map/ppermute | solution.py:294
  6.0 8.6 %collective-permute-done.3 = bf16[128,1024]{1,0:T(8,128)(2,1)S(1)} collective-permute-done((bf16[128,1024]{1,0:T(8,128)(2,1)}, bf16[128,1024]{1,0:T(8,128)(2,1)S(1)}, u32[]{:S(2)}, u32[]{:S(2)}) %collective-permute-start.3) | collective-permute-done | bytes 262176 | tf_op jit(solution)/shard_map/ppermute | solution.py:294
  14.6 19.9 %collective-permute-start.5 = (bf16[128,1024]{1,0:T(8,128)(2,1)S(1)}, bf16[128,1024]{1,0:T(8,128)(2,1)S(1)}, u32[]{:S(2)}, u32[]{:S(2)}) collective-permute-start(bf16[128,1024]{1,0:T(8,128)(2,1)S(1)} %collective-permute-done.3), channel_id=1, source_target_pairs={{16,32},{48,64},{80,96},{112,128},{144,160},{176,192},{208,224},{2... | collective-permute-start | bytes 786440 | tf_op jit(solution)/shard_map/ppermute | solution.py:291
  34.6 1.9 %collective-permute-start.4 = (bf16[128,1024]{1,0:T(8,128)(2,1)S(1)}, bf16[128,1024]{1,0:T(8,128)(2,1)}, u32[]{:S(2)}, u32[]{:S(2)}) collective-permute-start(bf16[128,1024]{1,0:T(8,128)(2,1)S(1)} %collective-permute-done.3), channel_id=1, source_target_pairs={{0,16},{32,48},{64,80},{96,112},{128,144},{160,176},{192,208},{224... | collective-permute-start | bytes 786440 | tf_op jit(solution)/shard_map/ppermute | solution.py:291
  36.5 2.8 %collective-permute-start.2 = (bf16[128,1024]{1,0:T(8,128)(2,1)}, bf16[128,1024]{1,0:T(8,128)(2,1)S(1)}, u32[]{:S(2)}, u32[]{:S(2)}) collective-permute-start(bf16[128,1024]{1,0:T(8,128)(2,1)} %slice.9), channel_id=1, source_target_pairs={{16,32},{48,64},{80,96},{112,128},{144,160},{176,192},{208,224},{2... | collective-permute-start | bytes 786440 | tf_op jit(solution)/shard_map/ppermute | solution.py:291
  39.3 7.0 %collective-permute-start.1 = (bf16[128,5120]{1,0:T(8,128)(2,1)}, bf16[128,5120]{1,0:T(8,128)(2,1)S(1)}, u32[]{:S(2)}, u32[]{:S(2)}) collective-permute-start(bf16[128,5120]{1,0:T(8,128)(2,1)} %bitcast.12), channel_id=1, source_target_pairs={{16,32},{48,64},{80,96},{112,128},{144,160},{176,192},{208,224},{2... | collective-permute-start | bytes 3932168 | tf_op jit(solution)/shard_map/ppermute | solution.py:291
  46.3 0.8 compare_bitcast_fusion.1
  47.1 0.1 broadcast_in_dim.63
  47.2 0.1 eq.96
  47.3 0.1 broadcast_in_dim.65
  47.4 0.1 eq.99
  47.4 0.1 broadcast_in_dim.61
  47.5 0.1 eq.93
  47.6 0.1 broadcast_in_dim.59
  47.7 0.1 eq.89
  47.8 0.0 collective-permute-done.5
  47.8 0.7 copy-done.4
  48.5 1.1 select_select_fusion.refs_5_
  49.6 3.4 %collective-permute-start.12 = (bf16[128,1024]{1,0:T(8,128)(2,1)S(1)}, bf16[128,1024]{1,0:T(8,128)(2,1)S(1)}, u32[]{:S(2)}, u32[]{:S(2)}) collective-permute-start(bf16[128,1024]{1,0:T(8,128)(2,1)S(1)} %select_select_fusion.refs_5_), channel_id=1, source_target_pairs={{0,2},{4,6},{8,10},{12,14},{2,0},{6,4},{10,8},{14,12},{1,3},{5,7},... | collective-permute-start | bytes 786440 | tf_op jit(solution)/shard_map/ppermute | solution.py:312
  53.0 3.9 %collective-permute-done.2 = bf16[128,1024]{1,0:T(8,128)(2,1)S(1)} collective-permute-done((bf16[128,1024]{1,0:T(8,128)(2,1)}, bf16[128,1024]{1,0:T(8,128)(2,1)S(1)}, u32[]{:S(2)}, u32[]{:S(2)}) %collective-permute-start.2) | collective-permute-done | bytes 262176 | tf_op jit(solution)/shard_map/ppermute | solution.py:291
  57.0 1.2 %slice_select_fusion.refs_4_ = bf16[128,1024]{1,0:T(8,128)(2,1)S(1)} fusion(bf16[128,5120]{1,0:T(8,128)(2,1)S(1)} %collective-permute-done.refs_2_, bf16[128,1024]{1,0:T(8,128)(2,1)S(1)} %collective-permute-done.2, pred[128]{0:T(512)(128)(4,1)S(1)} %eq.93, pred[128]{0:T(512)(128)(4,1)S(1)} %eq.89, bf16[128,5120]{1,0:T(8,128)(2,1)} %bitcast.13), kind=kLoop, calls=%fused_computation | loop fusion | flops 262144 | bytes 1048832 | tf_op jit(solution)/shard_map/jit(_where)/select_n | solution.py:304
  58.2 2.4 %collective-permute-start.7 = (bf16[128,1024]{1,0:T(8,128)(2,1)S(1)}, bf16[128,1024]{1,0:T(8,128)(2,1)S(1)}, u32[]{:S(2)}, u32[]{:S(2)}) collective-permute-start(bf16[128,1024]{1,0:T(8,128)(2,1)S(1)} %slice_select_fusion.refs_4_), channel_id=1, source_target_pairs={{2,4},{6,8},{10,12},{14,0},{4,2},{8,6},{12,10},{0,14},{3,5},{7,9},... | collective-permute-start | bytes 786440 | tf_op jit(solution)/shard_map/ppermute | solution.py:312
  60.7 3.4 %collective-permute-start.13 = (bf16[128,1024]{1,0:T(8,128)(2,1)S(1)}, bf16[128,1024]{1,0:T(8,128)(2,1)S(1)}, u32[]{:S(2)}, u32[]{:S(2)}) collective-permute-start(bf16[128,1024]{1,0:T(8,128)(2,1)S(1)} %select_select_fusion.refs_5_), channel_id=1, source_target_pairs={{2,4},{6,8},{10,12},{14,0},{4,2},{8,6},{12,10},{0,14},{3,5},{7,9},... | collective-permute-start | bytes 786440 | tf_op jit(solution)/shard_map/ppermute | solution.py:312
  64.1 0.0 collective-permute-done.12.refs_12_
  64.1 2.4 %collective-permute-start.15 = (bf16[128,1024]{1,0:T(8,128)(2,1)S(1)}, bf16[128,1024]{1,0:T(8,128)(2,1)S(1)}, u32[]{:S(2)}, u32[]{:S(2)}) collective-permute-start(bf16[128,1024]{1,0:T(8,128)(2,1)S(1)} %collective-permute-done.12.refs_12_), channel_id=1, source_target_pairs={{2,4},{6,8},{10,12},{14,0},{4,2},{8,6},{12,10},{0,14},{3,5},{7,9},... | collective-permute-start | bytes 786440 | tf_op jit(solution)/shard_map/ppermute | solution.py:312
  66.5 6.8 %collective-permute-start.6 = (bf16[128,1024]{1,0:T(8,128)(2,1)S(1)}, bf16[128,1024]{1,0:T(8,128)(2,1)S(1)}, u32[]{:S(2)}, u32[]{:S(2)}) collective-permute-start(bf16[128,1024]{1,0:T(8,128)(2,1)S(1)} %slice_select_fusion.refs_4_), channel_id=1, source_target_pairs={{0,2},{4,6},{8,10},{12,14},{2,0},{6,4},{10,8},{14,12},{1,3},{5,7},... | collective-permute-start | bytes 786440 | tf_op jit(solution)/shard_map/ppermute | solution.py:312
  73.3 0.0 collective-permute-done.7.refs_7_
  73.3 1.9 %collective-permute-start.8 = (bf16[128,1024]{1,0:T(8,128)(2,1)S(1)}, bf16[128,1024]{1,0:T(8,128)(2,1)S(1)}, u32[]{:S(2)}, u32[]{:S(2)}) collective-permute-start(bf16[128,1024]{1,0:T(8,128)(2,1)S(1)} %collective-permute-done.7.refs_7_), channel_id=1, source_target_pairs={{0,2},{4,6},{8,10},{12,14},{2,0},{6,4},{10,8},{14,12},{1,3},{5,7},... | collective-permute-start | bytes 786440 | tf_op jit(solution)/shard_map/ppermute | solution.py:312
  75.3 3.9 %collective-permute-start.14 = (bf16[128,1024]{1,0:T(8,128)(2,1)S(1)}, bf16[128,1024]{1,0:T(8,128)(2,1)}, u32[]{:S(2)}, u32[]{:S(2)}) collective-permute-start(bf16[128,1024]{1,0:T(8,128)(2,1)S(1)} %collective-permute-done.13.refs_13_), channel_id=1, source_target_pairs={{0,2},{4,6},{8,10},{12,14},{2,0},{6,4},{10,8},{14,12},{1,3},{5,7},... | collective-permute-start | bytes 786440 | tf_op jit(solution)/shard_map/ppermute | solution.py:312
  79.2 0.0 collective-permute-done.15.refs_15_
  79.2 1.9 %collective-permute-start.16 = (bf16[128,1024]{1,0:T(8,128)(2,1)S(1)}, bf16[128,1024]{1,0:T(8,128)(2,1)}, u32[]{:S(2)}, u32[]{:S(2)}) collective-permute-start(bf16[128,1024]{1,0:T(8,128)(2,1)S(1)} %collective-permute-done.15.refs_15_), channel_id=1, source_target_pairs={{0,2},{4,6},{8,10},{12,14},{2,0},{6,4},{10,8},{14,12},{1,3},{5,7},... | collective-permute-start | bytes 786440 | tf_op jit(solution)/shard_map/ppermute | solution.py:312
  81.2 0.0 collective-permute-done.6.refs_6_
  81.2 1.9 %collective-permute-start.9 = (bf16[128,1024]{1,0:T(8,128)(2,1)S(1)}, bf16[128,1024]{1,0:T(8,128)(2,1)}, u32[]{:S(2)}, u32[]{:S(2)}) collective-permute-start(bf16[128,1024]{1,0:T(8,128)(2,1)S(1)} %collective-permute-done.6.refs_6_), channel_id=1, source_target_pairs={{2,4},{6,8},{10,12},{14,0},{4,2},{8,6},{12,10},{0,14},{3,5},{7,9},... | collective-permute-start | bytes 786440 | tf_op jit(solution)/shard_map/ppermute | solution.py:312
  83.1 0.0 collective-permute-done.8.refs_8_
  83.2 3.9 %collective-permute-start.11 = (bf16[128,1024]{1,0:T(8,128)(2,1)S(1)}, bf16[128,1024]{1,0:T(8,128)(2,1)}, u32[]{:S(2)}, u32[]{:S(2)}) collective-permute-start(bf16[128,1024]{1,0:T(8,128)(2,1)S(1)} %collective-permute-done.8.refs_8_), channel_id=1, source_target_pairs={{2,4},{6,8},{10,12},{14,0},{4,2},{8,6},{12,10},{0,14},{3,5},{7,9},... | collective-permute-start | bytes 786440 | tf_op jit(solution)/shard_map/ppermute | solution.py:312
  87.1 0.0 collective-permute-done.14.refs_14_
  87.1 1.9 %collective-permute-start.17 = (bf16[128,1024]{1,0:T(8,128)(2,1)}, bf16[128,1024]{1,0:T(8,128)(2,1)}, u32[]{:S(2)}, u32[]{:S(2)}) collective-permute-start(bf16[128,1024]{1,0:T(8,128)(2,1)} %collective-permute-done.14.refs_14_), channel_id=1, source_target_pairs={{2,4},{6,8},{10,12},{14,0},{4,2},{8,6},{12,10},{0,14},{3,5},{7,9},... | collective-permute-start | bytes 786440 | tf_op jit(solution)/shard_map/ppermute | solution.py:312
  89.0 0.0 collective-permute-done.16.refs_16_
  89.1 3.9 %collective-permute-start.19 = (bf16[128,1024]{1,0:T(8,128)(2,1)}, bf16[128,1024]{1,0:T(8,128)(2,1)}, u32[]{:S(2)}, u32[]{:S(2)}) collective-permute-start(bf16[128,1024]{1,0:T(8,128)(2,1)} %collective-permute-done.16.refs_16_), channel_id=1, source_target_pairs={{2,4},{6,8},{10,12},{14,0},{4,2},{8,6},{12,10},{0,14},{3,5},{7,9},... | collective-permute-start | bytes 786440 | tf_op jit(solution)/shard_map/ppermute | solution.py:312
  93.0 6.3 %collective-permute-start.10 = (bf16[128,1024]{1,0:T(8,128)(2,1)}, bf16[128,1024]{1,0:T(8,128)(2,1)}, u32[]{:S(2)}, u32[]{:S(2)}) collective-permute-start(bf16[128,1024]{1,0:T(8,128)(2,1)} %collective-permute-done.9.refs_9_), channel_id=1, source_target_pairs={{0,2},{4,6},{8,10},{12,14},{2,0},{6,4},{10,8},{14,12},{1,3},{5,7},... | collective-permute-start | bytes 786440 | tf_op jit(solution)/shard_map/ppermute | solution.py:312
  99.4 1.9 %collective-permute-start.18 = (bf16[128,1024]{1,0:T(8,128)(2,1)}, bf16[128,1024]{1,0:T(8,128)(2,1)}, u32[]{:S(2)}, u32[]{:S(2)}) collective-permute-start(bf16[128,1024]{1,0:T(8,128)(2,1)} %collective-permute-done.11.refs_11_), channel_id=1, source_target_pairs={{0,2},{4,6},{8,10},{12,14},{2,0},{6,4},{10,8},{14,12},{1,3},{5,7},... | collective-permute-start | bytes 786440 | tf_op jit(solution)/shard_map/ppermute | solution.py:312
  101.3 0.7 copy.5.lengths_ref
  102.0 0.6 compare_select_fusion.3.where_ref
  102.6 2.2 %list_spans.1.refs_0_ = s32[2,128]{1,0:T(2,128)} custom-call(s32[8]{0:T(128)} %compare_select_fusion.3.where_ref, s32[1,32]{1,0:T(1,128)} %dest_ref.1, s32[32]{0:T(128)} %order_ref.1, s32[64,8]{1,0:T(8,128)} %copy.5.lengths_ref), custom_call_target="tpu_custom_call" | custom-call | flops 4000000 | bytes 4000 | tf_op jit(solution)/shard_map/list_spans/pallas_call | solution.py:234
  104.9 3.0 %collective-permute-done.18.refs_18_ = bf16[128,1024]{1,0:T(8,128)(2,1)} collective-permute-done((bf16[128,1024]{1,0:T(8,128)(2,1)}, bf16[128,1024]{1,0:T(8,128)(2,1)}, u32[]{:S(2)}, u32[]{:S(2)}) %collective-permute-start.18) | collective-permute-done | bytes 262176 | tf_op jit(solution)/shard_map/ppermute | solution.py:312
  108.0 8.4 %attend.1 = bf16[128,4096]{1,0:T(8,128)(2,1)} custom-call(s32[2,128]{1,0:T(2,128)} %list_spans.1.refs_0_, bf16[128,5120]{1,0:T(8,128)(2,1)} %bitcast.14, bf16[128,5120]{1,0:T(8,128)(2,1)} %copy-done, bf16[128,5120]{1,0:T(8,128)(2,1)} %copy-done.1, bf16[128,1024]{1,0:T(8,128)(2,1)} %copy-done.3, bf16[128,1024]{1,0:T(8,128)(2,1)} %copy-done.2, ...), custom_call_target="tpu_custom_call" | custom-call | flops 1000000000 | bytes 4000000 | tf_op jit(solution)/shard_map/attend/pallas_call | solution.py:249
  (32 shorter events, 0.1 us)
Async XLA Ops:
  0.0 101.3 %copy-start.11 = (s32[64,8]{0,1:T(8,128)S(1)}, s32[64,8]{0,1:T(8,128)}, u32[]{:S(2)}) copy-start(s32[64,8]{0,1:T(8,128)} %param.7) | copy-start | bytes 6148
  0.0 57.0 %collective-permute-start = (bf16[128,5120]{1,0:T(8,128)(2,1)}, bf16[128,5120]{1,0:T(8,128)(2,1)S(1)}, u32[]{:S(2)}, u32[]{:S(2)}) collective-permute-start(bf16[128,5120]{1,0:T(8,128)(2,1)} %bitcast.10), channel_id=1, source_target_pairs={{0,16},{32,48},{64,80},{96,112},{128,144},{160,176},{192,208},{224... | collective-permute-start | bytes 3932168 | tf_op jit(solution)/shard_map/ppermute | solution.py:291
  3.7 10.9 %collective-permute-start.3 = (bf16[128,1024]{1,0:T(8,128)(2,1)}, bf16[128,1024]{1,0:T(8,128)(2,1)S(1)}, u32[]{:S(2)}, u32[]{:S(2)}) collective-permute-start(bf16[128,1024]{1,0:T(8,128)(2,1)} %slice.9), channel_id=1, source_target_pairs={{0,1},{1,0},{2,3},{3,2},{4,5},{5,4},{6,7},{7,6},{8,9},{9,8},{10,11... | collective-permute-start | bytes 786440 | tf_op jit(solution)/shard_map/ppermute | solution.py:294
  14.6 33.2 %collective-permute-start.5 = (bf16[128,1024]{1,0:T(8,128)(2,1)S(1)}, bf16[128,1024]{1,0:T(8,128)(2,1)S(1)}, u32[]{:S(2)}, u32[]{:S(2)}) collective-permute-start(bf16[128,1024]{1,0:T(8,128)(2,1)S(1)} %collective-permute-done.3), channel_id=1, source_target_pairs={{16,32},{48,64},{80,96},{112,128},{144,160},{176,192},{208,224},{2... | collective-permute-start | bytes 786440 | tf_op jit(solution)/shard_map/ppermute | solution.py:291
  34.6 13.9 %collective-permute-start.4 = (bf16[128,1024]{1,0:T(8,128)(2,1)S(1)}, bf16[128,1024]{1,0:T(8,128)(2,1)}, u32[]{:S(2)}, u32[]{:S(2)}) collective-permute-start(bf16[128,1024]{1,0:T(8,128)(2,1)S(1)} %collective-permute-done.3), channel_id=1, source_target_pairs={{0,16},{32,48},{64,80},{96,112},{128,144},{160,176},{192,208},{224... | collective-permute-start | bytes 786440 | tf_op jit(solution)/shard_map/ppermute | solution.py:291
  36.5 20.5 %collective-permute-start.2 = (bf16[128,1024]{1,0:T(8,128)(2,1)}, bf16[128,1024]{1,0:T(8,128)(2,1)S(1)}, u32[]{:S(2)}, u32[]{:S(2)}) collective-permute-start(bf16[128,1024]{1,0:T(8,128)(2,1)} %slice.9), channel_id=1, source_target_pairs={{16,32},{48,64},{80,96},{112,128},{144,160},{176,192},{208,224},{2... | collective-permute-start | bytes 786440 | tf_op jit(solution)/shard_map/ppermute | solution.py:291
  39.3 65.6 %collective-permute-start.1 = (bf16[128,5120]{1,0:T(8,128)(2,1)}, bf16[128,5120]{1,0:T(8,128)(2,1)S(1)}, u32[]{:S(2)}, u32[]{:S(2)}) collective-permute-start(bf16[128,5120]{1,0:T(8,128)(2,1)} %bitcast.12), channel_id=1, source_target_pairs={{16,32},{48,64},{80,96},{112,128},{144,160},{176,192},{208,224},{2... | collective-permute-start | bytes 3932168 | tf_op jit(solution)/shard_map/ppermute | solution.py:291
  47.8 0.7 copy-start.4
  49.6 58.3 %copy-start.2 = (bf16[128,1024]{1,0:T(8,128)(2,1)}, bf16[128,1024]{1,0:T(8,128)(2,1)S(1)}, u32[]{:S(2)}) copy-start(bf16[128,1024]{1,0:T(8,128)(2,1)S(1)} %select_select_fusion.refs_5_) | copy-start | bytes 786436
  49.6 14.4 %collective-permute-start.12 = (bf16[128,1024]{1,0:T(8,128)(2,1)S(1)}, bf16[128,1024]{1,0:T(8,128)(2,1)S(1)}, u32[]{:S(2)}, u32[]{:S(2)}) collective-permute-start(bf16[128,1024]{1,0:T(8,128)(2,1)S(1)} %select_select_fusion.refs_5_), channel_id=1, source_target_pairs={{0,2},{4,6},{8,10},{12,14},{2,0},{6,4},{10,8},{14,12},{1,3},{5,7},... | collective-permute-start | bytes 786440 | tf_op jit(solution)/shard_map/ppermute | solution.py:312
  57.0 51.0 %copy-start = (bf16[128,5120]{1,0:T(8,128)(2,1)}, bf16[128,5120]{1,0:T(8,128)(2,1)S(1)}, u32[]{:S(2)}) copy-start(bf16[128,5120]{1,0:T(8,128)(2,1)S(1)} %collective-permute-done.refs_2_) | copy-start | bytes 3932164
  58.2 49.8 %copy-start.3 = (bf16[128,1024]{1,0:T(8,128)(2,1)}, bf16[128,1024]{1,0:T(8,128)(2,1)S(1)}, u32[]{:S(2)}) copy-start(bf16[128,1024]{1,0:T(8,128)(2,1)S(1)} %slice_select_fusion.refs_4_) | copy-start | bytes 786436
  58.2 15.1 %collective-permute-start.7 = (bf16[128,1024]{1,0:T(8,128)(2,1)S(1)}, bf16[128,1024]{1,0:T(8,128)(2,1)S(1)}, u32[]{:S(2)}, u32[]{:S(2)}) collective-permute-start(bf16[128,1024]{1,0:T(8,128)(2,1)S(1)} %slice_select_fusion.refs_4_), channel_id=1, source_target_pairs={{2,4},{6,8},{10,12},{14,0},{4,2},{8,6},{12,10},{0,14},{3,5},{7,9},... | collective-permute-start | bytes 786440 | tf_op jit(solution)/shard_map/ppermute | solution.py:312
  60.7 14.6 %collective-permute-start.13 = (bf16[128,1024]{1,0:T(8,128)(2,1)S(1)}, bf16[128,1024]{1,0:T(8,128)(2,1)S(1)}, u32[]{:S(2)}, u32[]{:S(2)}) collective-permute-start(bf16[128,1024]{1,0:T(8,128)(2,1)S(1)} %select_select_fusion.refs_5_), channel_id=1, source_target_pairs={{2,4},{6,8},{10,12},{14,0},{4,2},{8,6},{12,10},{0,14},{3,5},{7,9},... | collective-permute-start | bytes 786440 | tf_op jit(solution)/shard_map/ppermute | solution.py:312
  64.1 17.1 %copy-start.5 = (bf16[128,1024]{1,0:T(8,128)(2,1)}, bf16[128,1024]{1,0:T(8,128)(2,1)S(1)}, u32[]{:S(2)}) copy-start(bf16[128,1024]{1,0:T(8,128)(2,1)S(1)} %collective-permute-done.12.refs_12_) | copy-start | bytes 786436
  64.1 15.1 %collective-permute-start.15 = (bf16[128,1024]{1,0:T(8,128)(2,1)S(1)}, bf16[128,1024]{1,0:T(8,128)(2,1)S(1)}, u32[]{:S(2)}, u32[]{:S(2)}) collective-permute-start(bf16[128,1024]{1,0:T(8,128)(2,1)S(1)} %collective-permute-done.12.refs_12_), channel_id=1, source_target_pairs={{2,4},{6,8},{10,12},{14,0},{4,2},{8,6},{12,10},{0,14},{3,5},{7,9},... | collective-permute-start | bytes 786440 | tf_op jit(solution)/shard_map/ppermute | solution.py:312
  66.5 14.6 %collective-permute-start.6 = (bf16[128,1024]{1,0:T(8,128)(2,1)S(1)}, bf16[128,1024]{1,0:T(8,128)(2,1)S(1)}, u32[]{:S(2)}, u32[]{:S(2)}) collective-permute-start(bf16[128,1024]{1,0:T(8,128)(2,1)S(1)} %slice_select_fusion.refs_4_), channel_id=1, source_target_pairs={{0,2},{4,6},{8,10},{12,14},{2,0},{6,4},{10,8},{14,12},{1,3},{5,7},... | collective-permute-start | bytes 786440 | tf_op jit(solution)/shard_map/ppermute | solution.py:312
  73.3 34.6 %copy-start.6 = (bf16[128,1024]{1,0:T(8,128)(2,1)}, bf16[128,1024]{1,0:T(8,128)(2,1)S(1)}, u32[]{:S(2)}) copy-start(bf16[128,1024]{1,0:T(8,128)(2,1)S(1)} %collective-permute-done.7.refs_7_) | copy-start | bytes 786436
  73.3 9.8 %collective-permute-start.8 = (bf16[128,1024]{1,0:T(8,128)(2,1)S(1)}, bf16[128,1024]{1,0:T(8,128)(2,1)S(1)}, u32[]{:S(2)}, u32[]{:S(2)}) collective-permute-start(bf16[128,1024]{1,0:T(8,128)(2,1)S(1)} %collective-permute-done.7.refs_7_), channel_id=1, source_target_pairs={{0,2},{4,6},{8,10},{12,14},{2,0},{6,4},{10,8},{14,12},{1,3},{5,7},... | collective-permute-start | bytes 786440 | tf_op jit(solution)/shard_map/ppermute | solution.py:312
  75.3 7.9 %copy-start.7 = (bf16[128,1024]{1,0:T(8,128)(2,1)}, bf16[128,1024]{1,0:T(8,128)(2,1)S(1)}, u32[]{:S(2)}) copy-start(bf16[128,1024]{1,0:T(8,128)(2,1)S(1)} %collective-permute-done.13.refs_13_) | copy-start | bytes 786436
  75.3 11.8 %collective-permute-start.14 = (bf16[128,1024]{1,0:T(8,128)(2,1)S(1)}, bf16[128,1024]{1,0:T(8,128)(2,1)}, u32[]{:S(2)}, u32[]{:S(2)}) collective-permute-start(bf16[128,1024]{1,0:T(8,128)(2,1)S(1)} %collective-permute-done.13.refs_13_), channel_id=1, source_target_pairs={{0,2},{4,6},{8,10},{12,14},{2,0},{6,4},{10,8},{14,12},{1,3},{5,7},... | collective-permute-start | bytes 786440 | tf_op jit(solution)/shard_map/ppermute | solution.py:312
  79.2 7.9 %copy-start.8 = (bf16[128,1024]{1,0:T(8,128)(2,1)}, bf16[128,1024]{1,0:T(8,128)(2,1)S(1)}, u32[]{:S(2)}) copy-start(bf16[128,1024]{1,0:T(8,128)(2,1)S(1)} %collective-permute-done.15.refs_15_) | copy-start | bytes 786436
  79.2 9.8 %collective-permute-start.16 = (bf16[128,1024]{1,0:T(8,128)(2,1)S(1)}, bf16[128,1024]{1,0:T(8,128)(2,1)}, u32[]{:S(2)}, u32[]{:S(2)}) collective-permute-start(bf16[128,1024]{1,0:T(8,128)(2,1)S(1)} %collective-permute-done.15.refs_15_), channel_id=1, source_target_pairs={{0,2},{4,6},{8,10},{12,14},{2,0},{6,4},{10,8},{14,12},{1,3},{5,7},... | collective-permute-start | bytes 786440 | tf_op jit(solution)/shard_map/ppermute | solution.py:312
  81.2 7.9 %copy-start.9 = (bf16[128,1024]{1,0:T(8,128)(2,1)}, bf16[128,1024]{1,0:T(8,128)(2,1)S(1)}, u32[]{:S(2)}) copy-start(bf16[128,1024]{1,0:T(8,128)(2,1)S(1)} %collective-permute-done.6.refs_6_) | copy-start | bytes 786436
  81.2 11.8 %collective-permute-start.9 = (bf16[128,1024]{1,0:T(8,128)(2,1)S(1)}, bf16[128,1024]{1,0:T(8,128)(2,1)}, u32[]{:S(2)}, u32[]{:S(2)}) collective-permute-start(bf16[128,1024]{1,0:T(8,128)(2,1)S(1)} %collective-permute-done.6.refs_6_), channel_id=1, source_target_pairs={{2,4},{6,8},{10,12},{14,0},{4,2},{8,6},{12,10},{0,14},{3,5},{7,9},... | collective-permute-start | bytes 786440 | tf_op jit(solution)/shard_map/ppermute | solution.py:312
  83.2 9.9 %copy-start.10 = (bf16[128,1024]{1,0:T(8,128)(2,1)}, bf16[128,1024]{1,0:T(8,128)(2,1)S(1)}, u32[]{:S(2)}) copy-start(bf16[128,1024]{1,0:T(8,128)(2,1)S(1)} %collective-permute-done.8.refs_8_) | copy-start | bytes 786436
  83.2 16.2 %collective-permute-start.11 = (bf16[128,1024]{1,0:T(8,128)(2,1)S(1)}, bf16[128,1024]{1,0:T(8,128)(2,1)}, u32[]{:S(2)}, u32[]{:S(2)}) collective-permute-start(bf16[128,1024]{1,0:T(8,128)(2,1)S(1)} %collective-permute-done.8.refs_8_), channel_id=1, source_target_pairs={{2,4},{6,8},{10,12},{14,0},{4,2},{8,6},{12,10},{0,14},{3,5},{7,9},... | collective-permute-start | bytes 786440 | tf_op jit(solution)/shard_map/ppermute | solution.py:312
  87.1 17.8 %collective-permute-start.17 = (bf16[128,1024]{1,0:T(8,128)(2,1)}, bf16[128,1024]{1,0:T(8,128)(2,1)}, u32[]{:S(2)}, u32[]{:S(2)}) collective-permute-start(bf16[128,1024]{1,0:T(8,128)(2,1)} %collective-permute-done.14.refs_14_), channel_id=1, source_target_pairs={{2,4},{6,8},{10,12},{14,0},{4,2},{8,6},{12,10},{0,14},{3,5},{7,9},... | collective-permute-start | bytes 786440 | tf_op jit(solution)/shard_map/ppermute | solution.py:312
  89.1 15.8 %collective-permute-start.19 = (bf16[128,1024]{1,0:T(8,128)(2,1)}, bf16[128,1024]{1,0:T(8,128)(2,1)}, u32[]{:S(2)}, u32[]{:S(2)}) collective-permute-start(bf16[128,1024]{1,0:T(8,128)(2,1)} %collective-permute-done.16.refs_16_), channel_id=1, source_target_pairs={{2,4},{6,8},{10,12},{14,0},{4,2},{8,6},{12,10},{0,14},{3,5},{7,9},... | collective-permute-start | bytes 786440 | tf_op jit(solution)/shard_map/ppermute | solution.py:312
  93.0 11.9 %collective-permute-start.10 = (bf16[128,1024]{1,0:T(8,128)(2,1)}, bf16[128,1024]{1,0:T(8,128)(2,1)}, u32[]{:S(2)}, u32[]{:S(2)}) collective-permute-start(bf16[128,1024]{1,0:T(8,128)(2,1)} %collective-permute-done.9.refs_9_), channel_id=1, source_target_pairs={{0,2},{4,6},{8,10},{12,14},{2,0},{6,4},{10,8},{14,12},{1,3},{5,7},... | collective-permute-start | bytes 786440 | tf_op jit(solution)/shard_map/ppermute | solution.py:312
  99.4 8.6 %collective-permute-start.18 = (bf16[128,1024]{1,0:T(8,128)(2,1)}, bf16[128,1024]{1,0:T(8,128)(2,1)}, u32[]{:S(2)}, u32[]{:S(2)}) collective-permute-start(bf16[128,1024]{1,0:T(8,128)(2,1)} %collective-permute-done.11.refs_11_), channel_id=1, source_target_pairs={{0,2},{4,6},{8,10},{12,14},{2,0},{6,4},{10,8},{14,12},{1,3},{5,7},... | collective-permute-start | bytes 786440 | tf_op jit(solution)/shard_map/ppermute | solution.py:312
  104.9 3.1 %copy-start.1 = (bf16[128,5120]{1,0:T(8,128)(2,1)}, bf16[128,5120]{1,0:T(8,128)(2,1)S(1)}, u32[]{:S(2)}) copy-start(bf16[128,5120]{1,0:T(8,128)(2,1)S(1)} %collective-permute-done.1.refs_3_) | copy-start | bytes 3932164

commit v2 on v0

--- a/solution.py
+++ b/solution.py
@@ -115,6 +115,13 @@
             ),
         )
 
+    def for_wanted(act):
+        for index in range(SPANS):
+
+            @pl.when(plan[0, WANTED + index] + plan[1, WANTED + index] > 0)
+            def _(index=index):
+                act(piece_copies(index))
+
     for half in range(2):
         for which in range(3):
 
@@ -122,22 +129,9 @@
             def _(half=half, which=which):
                 query_copy(half, which).start()
 
-    for index in range(SPANS):
-
-        @pl.when(plan[0, WANTED + index] + plan[1, WANTED + index] > 0)
-        def _(index=index):
-            for copy in piece_copies(index):
-                copy.start()
-
-    for half in range(2):
-        query_copy(half, 0).wait()
-    for index in range(SPANS):
-
-        @pl.when(plan[0, WANTED + index] + plan[1, WANTED + index] > 0)
-        def _(index=index):
-            for copy in piece_copies(index):
-                copy.wait()
-
+        for_wanted(lambda copies: copies[half].start())
+
+    for_wanted(lambda copies: copies[0].wait())
     lane = lax.broadcasted_iota(jnp.int32, (1, CHUNK * SPAN), 1)
     rows = QUERIES_PER_KV * SPAN
 
@@ -148,6 +142,7 @@
             end = plan[half, ENDS + doc]
             start = jnp.where(position >= end, end, start)
         chunks = plan[half, CHUNKS]
+        query_copy(half, 0).wait()
         peaks[...] = jnp.full_like(peaks, MASK_FLOOR)
         sums[...] = jnp.zeros_like(sums)
         mixed[...] = jnp.zeros_like(mixed)
@@ -194,6 +189,10 @@
             peaks[group] = jnp.broadcast_to(
                 jnp.max(peaks[group], axis=1, keepdims=True), (rows, HEAD_SIZE)
             )
+
+        @pl.when(half == 0)
+        def _():
+            for_wanted(lambda copies: copies[1].wait())
 
         def mix_chunk(chunk, carry):
             firsts_of = first_rows(chunk)

time: 107 us -> 107 us (level)
  no operation moved by 1% of the time
where the time goes in v2:
time: 107 us; the launch traced here: 106 us
  starting transfers between devices  78.1 us (73%)
  waiting for transfers between devices  13.2 us (12%)
  Pallas kernels  9.55 us (9%)
  other arithmetic  2.44 us (2%)
  local copies, waits for them, and re-layouts  2.04 us (2%)
    ppermute x14, starting transfers between devices, across(): return lax.ppermute(array, 'ctx_0', swaps(columns, first))  44.5 us
    ppermute x3, starting transfers between devices, trade(): return lax.ppermute(array, 'dp', swaps(dp_count, first))  30.7 us
    ppermute x14, waiting for transfers between devices, across(): return lax.ppermute(array, 'ctx_0', swaps(columns, first))  7.42 us
    pallas_call x1, Pallas kernels, attention(): pl.pallas_call(functools.partial(attention_kernel, pieces, count), out_sh...  7.3 us
    ppermute x3, waiting for transfers between devices, trade(): return lax.ppermute(array, 'dp', swaps(dp_count, first))  5.77 us
    ppermute x1, starting transfers between devices, on_device(): other = lax.ppermute(own, 'ctx_1', [(0, 1), (1, 0)])  3 us
    pallas_call x1, Pallas kernels, list_key_spans(): pl.pallas_call(functools.partial(list_kernel, pieces), out_shape=jax.Shap...  2.25 us
  transfers between devices with their start and end apart: 18, of which 5 were waited for; matrix products, arithmetic and copies ran while one was open for 3% of the time, Pallas kernels for 2%

profile of v2, /device:TPU:22, one launch (start us, length us, event | category | flops | bytes accessed | tf_op | source)
XLA Modules:
  0.0 105.8 jit_solution(17307863210179383215)
XLA Ops:
  0.0 2.0 %collective-permute-start = (bf16[128,5120]{1,0:T(8,128)(2,1)}, bf16[128,5120]{1,0:T(8,128)(2,1)S(1)}, u32[]{:S(2)}, u32[]{:S(2)}) collective-permute-start(bf16[128,5120]{1,0:T(8,128)(2,1)} %bitcast.6), channel_id=1, source_target_pairs={{0,16},{32,48},{64,80},{96,112},{128,144},{160,176},{192,208},{224... | collective-permute-start | bytes 3932168 | tf_op jit(solution)/shard_map/ppermute | solution.py:290
  2.1 1.0 slice.9
  3.0 20.9 %collective-permute-start.2 = (bf16[128,1024]{1,0:T(8,128)(2,1)S(1)}, bf16[128,1024]{1,0:T(8,128)(2,1)S(1)}, u32[]{:S(2)}, u32[]{:S(2)}) collective-permute-start(bf16[128,1024]{1,0:T(8,128)(2,1)S(1)} %slice.9), channel_id=1, source_target_pairs={{16,32},{48,64},{80,96},{112,128},{144,160},{176,192},{208,224},{2... | collective-permute-start | bytes 786440 | tf_op jit(solution)/shard_map/ppermute | solution.py:290
  24.0 0.7 compare_bitcast_fusion.1
  24.7 0.1 broadcast_in_dim.44
  24.8 0.1 eq.57
  24.8 0.1 broadcast_in_dim.46
  24.9 0.1 eq.61
  25.0 5.8 %collective-permute-done.2 = bf16[128,1024]{1,0:T(8,128)(2,1)S(1)} collective-permute-done((bf16[128,1024]{1,0:T(8,128)(2,1)S(1)}, bf16[128,1024]{1,0:T(8,128)(2,1)S(1)}, u32[]{:S(2)}, u32[]{:S(2)}) %collective-permute-start.2) | collective-permute-done | bytes 262176 | tf_op jit(solution)/shard_map/ppermute | solution.py:290
  30.8 0.0 collective-permute-done.refs_2_
  30.8 1.2 %slice_select_fusion.refs_4_ = bf16[128,1024]{1,0:T(8,128)(2,1)S(1)} fusion(bf16[128,5120]{1,0:T(8,128)(2,1)S(1)} %collective-permute-done.refs_2_, bf16[128,1024]{1,0:T(8,128)(2,1)S(1)} %collective-permute-done.2, pred[128]{0:T(512)(128)(4,1)S(1)} %eq.61, pred[128]{0:T(512)(128)(4,1)S(1)} %eq.57, bf16[128,5120]{1,0:T(8,128)(2,1)} %bitcast.8), kind=kLoop, calls=%fused_computation | loop fusion | flops 262144 | bytes 1048832 | tf_op jit(solution)/shard_map/jit(_where)/select_n | solution.py:299
  32.0 3.0 %collective-permute-start.3 = (bf16[128,1024]{1,0:T(8,128)(2,1)S(1)}, bf16[128,1024]{1,0:T(8,128)(2,1)S(1)}, u32[]{:S(2)}, u32[]{:S(2)}) collective-permute-start(bf16[128,1024]{1,0:T(8,128)(2,1)S(1)} %slice_select_fusion.refs_4_), channel_id=1, source_target_pairs={{0,1},{1,0},{2,3},{3,2},{4,5},{5,4},{6,7},{7,6},{8,9},{9,8},{10,11... | collective-permute-start | bytes 786440 | tf_op jit(solution)/shard_map/ppermute | solution.py:302
  35.0 7.7 %collective-permute-start.1 = (bf16[128,5120]{1,0:T(8,128)(2,1)S(1)}, bf16[128,5120]{1,0:T(8,128)(2,1)}, u32[]{:S(2)}, u32[]{:S(2)}) collective-permute-start(bf16[128,5120]{1,0:T(8,128)(2,1)S(1)} %bitcast.10), channel_id=1, source_target_pairs={{16,32},{48,64},{80,96},{112,128},{144,160},{176,192},{208,224},{2... | collective-permute-start | bytes 3932168 | tf_op jit(solution)/shard_map/ppermute | solution.py:290
  42.8 4.6 %collective-permute-start.5 = (bf16[128,1024]{1,0:T(8,128)(2,1)S(1)}, bf16[128,1024]{1,0:T(8,128)(2,1)S(1)}, u32[]{:S(2)}, u32[]{:S(2)}) collective-permute-start(bf16[128,1024]{1,0:T(8,128)(2,1)S(1)} %slice_select_fusion.refs_4_), channel_id=1, source_target_pairs={{2,4},{6,8},{10,12},{14,0},{4,2},{8,6},{12,10},{0,14},{3,5},{7,9},... | collective-permute-start | bytes 786440 | tf_op jit(solution)/shard_map/ppermute | solution.py:305
  47.4 0.0 collective-permute-done.3.refs_5_
  47.4 1.9 %collective-permute-start.10 = (bf16[128,1024]{1,0:T(8,128)(2,1)S(1)}, bf16[128,1024]{1,0:T(8,128)(2,1)S(1)}, u32[]{:S(2)}, u32[]{:S(2)}) collective-permute-start(bf16[128,1024]{1,0:T(8,128)(2,1)S(1)} %collective-permute-done.3.refs_5_), channel_id=1, source_target_pairs={{0,2},{4,6},{8,10},{12,14},{2,0},{6,4},{10,8},{14,12},{1,3},{5,7},... | collective-permute-start | bytes 786440 | tf_op jit(solution)/shard_map/ppermute | solution.py:305
  49.3 3.9 %collective-permute-start.4 = (bf16[128,1024]{1,0:T(8,128)(2,1)S(1)}, bf16[128,1024]{1,0:T(8,128)(2,1)S(1)}, u32[]{:S(2)}, u32[]{:S(2)}) collective-permute-start(bf16[128,1024]{1,0:T(8,128)(2,1)S(1)} %slice_select_fusion.refs_4_), channel_id=1, source_target_pairs={{0,2},{4,6},{8,10},{12,14},{2,0},{6,4},{10,8},{14,12},{1,3},{5,7},... | collective-permute-start | bytes 786440 | tf_op jit(solution)/shard_map/ppermute | solution.py:305
  53.3 0.0 collective-permute-done.5.refs_7_
  53.3 3.0 %collective-permute-start.6 = (bf16[128,1024]{1,0:T(8,128)(2,1)S(1)}, bf16[128,1024]{1,0:T(8,128)(2,1)S(1)}, u32[]{:S(2)}, u32[]{:S(2)}) collective-permute-start(bf16[128,1024]{1,0:T(8,128)(2,1)S(1)} %collective-permute-done.5.refs_7_), channel_id=1, source_target_pairs={{0,2},{4,6},{8,10},{12,14},{2,0},{6,4},{10,8},{14,12},{1,3},{5,7},... | collective-permute-start | bytes 786440 | tf_op jit(solution)/shard_map/ppermute | solution.py:305
  56.3 4.7 %collective-permute-start.11 = (bf16[128,1024]{1,0:T(8,128)(2,1)S(1)}, bf16[128,1024]{1,0:T(8,128)(2,1)S(1)}, u32[]{:S(2)}, u32[]{:S(2)}) collective-permute-start(bf16[128,1024]{1,0:T(8,128)(2,1)S(1)} %collective-permute-done.3.refs_5_), channel_id=1, source_target_pairs={{2,4},{6,8},{10,12},{14,0},{4,2},{8,6},{12,10},{0,14},{3,5},{7,9},... | collective-permute-start | bytes 786440 | tf_op jit(solution)/shard_map/ppermute | solution.py:305
  61.0 0.0 collective-permute-done.10.refs_12_
  61.0 2.4 %collective-permute-start.13 = (bf16[128,1024]{1,0:T(8,128)(2,1)S(1)}, bf16[128,1024]{1,0:T(8,128)(2,1)S(1)}, u32[]{:S(2)}, u32[]{:S(2)}) collective-permute-start(bf16[128,1024]{1,0:T(8,128)(2,1)S(1)} %collective-permute-done.10.refs_12_), channel_id=1, source_target_pairs={{2,4},{6,8},{10,12},{14,0},{4,2},{8,6},{12,10},{0,14},{3,5},{7,9},... | collective-permute-start | bytes 786440 | tf_op jit(solution)/shard_map/ppermute | solution.py:305
  63.4 0.7 collective-permute-done.4.refs_6_
  64.1 4.0 %collective-permute-start.7 = (bf16[128,1024]{1,0:T(8,128)(2,1)S(1)}, bf16[128,1024]{1,0:T(8,128)(2,1)}, u32[]{:S(2)}, u32[]{:S(2)}) collective-permute-start(bf16[128,1024]{1,0:T(8,128)(2,1)S(1)} %collective-permute-done.4.refs_6_), channel_id=1, source_target_pairs={{2,4},{6,8},{10,12},{14,0},{4,2},{8,6},{12,10},{0,14},{3,5},{7,9},... | collective-permute-start | bytes 786440 | tf_op jit(solution)/shard_map/ppermute | solution.py:305
  68.1 1.6 %collective-permute-done.6.refs_8_ = bf16[128,1024]{1,0:T(8,128)(2,1)S(1)} collective-permute-done((bf16[128,1024]{1,0:T(8,128)(2,1)S(1)}, bf16[128,1024]{1,0:T(8,128)(2,1)S(1)}, u32[]{:S(2)}, u32[]{:S(2)}) %collective-permute-start.6) | collective-permute-done | bytes 262176 | tf_op jit(solution)/shard_map/ppermute | solution.py:305
  69.7 1.9 %collective-permute-start.9 = (bf16[128,1024]{1,0:T(8,128)(2,1)S(1)}, bf16[128,1024]{1,0:T(8,128)(2,1)}, u32[]{:S(2)}, u32[]{:S(2)}) collective-permute-start(bf16[128,1024]{1,0:T(8,128)(2,1)S(1)} %collective-permute-done.6.refs_8_), channel_id=1, source_target_pairs={{2,4},{6,8},{10,12},{14,0},{4,2},{8,6},{12,10},{0,14},{3,5},{7,9},... | collective-permute-start | bytes 786440 | tf_op jit(solution)/shard_map/ppermute | solution.py:305
  71.6 0.0 collective-permute-done.11.refs_13_
  71.7 0.0 copy-done.5
  71.7 1.9 %collective-permute-start.12 = (bf16[128,1024]{1,0:T(8,128)(2,1)S(1)}, bf16[128,1024]{1,0:T(8,128)(2,1)}, u32[]{:S(2)}, u32[]{:S(2)}) collective-permute-start(bf16[128,1024]{1,0:T(8,128)(2,1)S(1)} %collective-permute-done.11.refs_13_), channel_id=1, source_target_pairs={{0,2},{4,6},{8,10},{12,14},{2,0},{6,4},{10,8},{14,12},{1,3},{5,7},... | collective-permute-start | bytes 786440 | tf_op jit(solution)/shard_map/ppermute | solution.py:305
  73.6 0.0 collective-permute-done.13.refs_15_
  73.6 3.9 %collective-permute-start.14 = (bf16[128,1024]{1,0:T(8,128)(2,1)S(1)}, bf16[128,1024]{1,0:T(8,128)(2,1)}, u32[]{:S(2)}, u32[]{:S(2)}) collective-permute-start(bf16[128,1024]{1,0:T(8,128)(2,1)S(1)} %collective-permute-done.13.refs_15_), channel_id=1, source_target_pairs={{0,2},{4,6},{8,10},{12,14},{2,0},{6,4},{10,8},{14,12},{1,3},{5,7},... | collective-permute-start | bytes 786440 | tf_op jit(solution)/shard_map/ppermute | solution.py:305
  77.6 0.0 collective-permute-done.7.refs_9_
  77.6 1.9 %collective-permute-start.8 = (bf16[128,1024]{1,0:T(8,128)(2,1)}, bf16[128,1024]{1,0:T(8,128)(2,1)}, u32[]{:S(2)}, u32[]{:S(2)}) collective-permute-start(bf16[128,1024]{1,0:T(8,128)(2,1)} %collective-permute-done.7.refs_9_), channel_id=1, source_target_pairs={{0,2},{4,6},{8,10},{12,14},{2,0},{6,4},{10,8},{14,12},{1,3},{5,7},... | collective-permute-start | bytes 786440 | tf_op jit(solution)/shard_map/ppermute | solution.py:305
  79.5 0.6 collective-permute-done.9.refs_11_
  80.2 3.3 %collective-permute-start.16 = (bf16[128,1024]{1,0:T(8,128)(2,1)}, bf16[128,1024]{1,0:T(8,128)(2,1)}, u32[]{:S(2)}, u32[]{:S(2)}) collective-permute-start(bf16[128,1024]{1,0:T(8,128)(2,1)} %collective-permute-done.9.refs_11_), channel_id=1, source_target_pairs={{0,2},{4,6},{8,10},{12,14},{2,0},{6,4},{10,8},{14,12},{1,3},{5,7},... | collective-permute-start | bytes 786440 | tf_op jit(solution)/shard_map/ppermute | solution.py:305
  83.5 0.0 collective-permute-done.12.refs_14_
  83.5 5.1 %collective-permute-start.15 = (bf16[128,1024]{1,0:T(8,128)(2,1)}, bf16[128,1024]{1,0:T(8,128)(2,1)}, u32[]{:S(2)}, u32[]{:S(2)}) collective-permute-start(bf16[128,1024]{1,0:T(8,128)(2,1)} %collective-permute-done.12.refs_14_), channel_id=1, source_target_pairs={{2,4},{6,8},{10,12},{14,0},{4,2},{8,6},{12,10},{0,14},{3,5},{7,9},... | collective-permute-start | bytes 786440 | tf_op jit(solution)/shard_map/ppermute | solution.py:305
  88.6 0.0 collective-permute-done.14.refs_16_
  88.6 1.9 %collective-permute-start.17 = (bf16[128,1024]{1,0:T(8,128)(2,1)}, bf16[128,1024]{1,0:T(8,128)(2,1)}, u32[]{:S(2)}, u32[]{:S(2)}) collective-permute-start(bf16[128,1024]{1,0:T(8,128)(2,1)} %collective-permute-done.14.refs_16_), channel_id=1, source_target_pairs={{2,4},{6,8},{10,12},{14,0},{4,2},{8,6},{12,10},{0,14},{3,5},{7,9},... | collective-permute-start | bytes 786440 | tf_op jit(solution)/shard_map/ppermute | solution.py:305
  90.6 0.7 copy.5.lengths_ref
  91.3 0.5 compare_select_fusion.3.where_ref
  91.8 2.2 %list_spans.1.refs_0_ = s32[2,128]{1,0:T(2,128)} custom-call(s32[8]{0:T(128)} %compare_select_fusion.3.where_ref, s32[1,32]{1,0:T(1,128)} %dest_ref.1, s32[32]{0:T(128)} %order_ref.1, s32[64,8]{1,0:T(8,128)} %copy.5.lengths_ref), custom_call_target="tpu_custom_call" | custom-call | flops 4000000 | bytes 4000 | tf_op jit(solution)/shard_map/list_spans/pallas_call | solution.py:233
  94.0 0.0 collective-permute-done.1.refs_3_
  94.0 0.0 collective-permute-done.8.refs_10_
  94.0 0.0 collective-permute-done.16.refs_18_
  94.1 0.0 collective-permute-done.15.refs_17_
  94.1 4.4 %collective-permute-done.17.refs_19_ = bf16[128,1024]{1,0:T(8,128)(2,1)} collective-permute-done((bf16[128,1024]{1,0:T(8,128)(2,1)}, bf16[128,1024]{1,0:T(8,128)(2,1)}, u32[]{:S(2)}, u32[]{:S(2)}) %collective-permute-start.17) | collective-permute-done | bytes 262176 | tf_op jit(solution)/shard_map/ppermute | solution.py:305
  98.5 7.3 %attend.1 = bf16[128,4096]{1,0:T(8,128)(2,1)} custom-call(s32[2,128]{1,0:T(2,128)} %list_spans.1.refs_0_, bf16[128,5120]{1,0:T(8,128)(2,1)} %bitcast.9, bf16[128,5120]{1,0:T(8,128)(2,1)} %copy-done.1, bf16[128,5120]{1,0:T(8,128)(2,1)} %collective-permute-done.1.refs_3_, bf16[128,1024]{1,0:T(8,128)(2,1)} %copy-done.2, bf16[128,1024]{1,0:T(8,128)(2,1)} %copy-done.3, ...), custom_call_target="tpu_custom_call" | custom-call | flops 1000000000 | bytes 4000000 | tf_op jit(solution)/shard_map/attend/pallas_call | solution.py:248
  (21 shorter events, 0.0 us)
Async XLA Ops:
  0.0 35.0 %copy-start = (bf16[1,128,5120]{2,1,0:T(8,128)(2,1)S(1)}, bf16[1,128,5120]{2,1,0:T(8,128)(2,1)}, u32[]{:S(2)}) copy-start(bf16[1,128,5120]{2,1,0:T(8,128)(2,1)} %param.4) | copy-start | bytes 3932164
  0.0 90.6 %copy-start.10 = (s32[64,8]{0,1:T(8,128)S(1)}, s32[64,8]{0,1:T(8,128)}, u32[]{:S(2)}) copy-start(s32[64,8]{0,1:T(8,128)} %param.7) | copy-start | bytes 6148
  0.0 30.8 %collective-permute-start = (bf16[128,5120]{1,0:T(8,128)(2,1)}, bf16[128,5120]{1,0:T(8,128)(2,1)S(1)}, u32[]{:S(2)}, u32[]{:S(2)}) collective-permute-start(bf16[128,5120]{1,0:T(8,128)(2,1)} %bitcast.6), channel_id=1, source_target_pairs={{0,16},{32,48},{64,80},{96,112},{128,144},{160,176},{192,208},{224... | collective-permute-start | bytes 3932168 | tf_op jit(solution)/shard_map/ppermute | solution.py:290
  3.0 27.7 %collective-permute-start.2 = (bf16[128,1024]{1,0:T(8,128)(2,1)S(1)}, bf16[128,1024]{1,0:T(8,128)(2,1)S(1)}, u32[]{:S(2)}, u32[]{:S(2)}) collective-permute-start(bf16[128,1024]{1,0:T(8,128)(2,1)S(1)} %slice.9), channel_id=1, source_target_pairs={{16,32},{48,64},{80,96},{112,128},{144,160},{176,192},{208,224},{2... | collective-permute-start | bytes 786440 | tf_op jit(solution)/shard_map/ppermute | solution.py:290
  30.8 67.7 %copy-start.1 = (bf16[128,5120]{1,0:T(8,128)(2,1)}, bf16[128,5120]{1,0:T(8,128)(2,1)S(1)}, u32[]{:S(2)}) copy-start(bf16[128,5120]{1,0:T(8,128)(2,1)S(1)} %collective-permute-done.refs_2_) | copy-start | bytes 3932164
  32.0 66.4 %copy-start.2 = (bf16[128,1024]{1,0:T(8,128)(2,1)}, bf16[128,1024]{1,0:T(8,128)(2,1)S(1)}, u32[]{:S(2)}) copy-start(bf16[128,1024]{1,0:T(8,128)(2,1)S(1)} %slice_select_fusion.refs_4_) | copy-start | bytes 786436
  32.0 15.4 %collective-permute-start.3 = (bf16[128,1024]{1,0:T(8,128)(2,1)S(1)}, bf16[128,1024]{1,0:T(8,128)(2,1)S(1)}, u32[]{:S(2)}, u32[]{:S(2)}) collective-permute-start(bf16[128,1024]{1,0:T(8,128)(2,1)S(1)} %slice_select_fusion.refs_4_), channel_id=1, source_target_pairs={{0,1},{1,0},{2,3},{3,2},{4,5},{5,4},{6,7},{7,6},{8,9},{9,8},{10,11... | collective-permute-start | bytes 786440 | tf_op jit(solution)/shard_map/ppermute | solution.py:302
  35.0 59.0 %collective-permute-start.1 = (bf16[128,5120]{1,0:T(8,128)(2,1)S(1)}, bf16[128,5120]{1,0:T(8,128)(2,1)}, u32[]{:S(2)}, u32[]{:S(2)}) collective-permute-start(bf16[128,5120]{1,0:T(8,128)(2,1)S(1)} %bitcast.10), channel_id=1, source_target_pairs={{16,32},{48,64},{80,96},{112,128},{144,160},{176,192},{208,224},{2... | collective-permute-start | bytes 3932168 | tf_op jit(solution)/shard_map/ppermute | solution.py:290
  42.8 10.5 %collective-permute-start.5 = (bf16[128,1024]{1,0:T(8,128)(2,1)S(1)}, bf16[128,1024]{1,0:T(8,128)(2,1)S(1)}, u32[]{:S(2)}, u32[]{:S(2)}) collective-permute-start(bf16[128,1024]{1,0:T(8,128)(2,1)S(1)} %slice_select_fusion.refs_4_), channel_id=1, source_target_pairs={{2,4},{6,8},{10,12},{14,0},{4,2},{8,6},{12,10},{0,14},{3,5},{7,9},... | collective-permute-start | bytes 786440 | tf_op jit(solution)/shard_map/ppermute | solution.py:305
  47.4 51.0 %copy-start.3 = (bf16[128,1024]{1,0:T(8,128)(2,1)}, bf16[128,1024]{1,0:T(8,128)(2,1)S(1)}, u32[]{:S(2)}) copy-start(bf16[128,1024]{1,0:T(8,128)(2,1)S(1)} %collective-permute-done.3.refs_5_) | copy-start | bytes 786436
  47.4 13.6 %collective-permute-start.10 = (bf16[128,1024]{1,0:T(8,128)(2,1)S(1)}, bf16[128,1024]{1,0:T(8,128)(2,1)S(1)}, u32[]{:S(2)}, u32[]{:S(2)}) collective-permute-start(bf16[128,1024]{1,0:T(8,128)(2,1)S(1)} %collective-permute-done.3.refs_5_), channel_id=1, source_target_pairs={{0,2},{4,6},{8,10},{12,14},{2,0},{6,4},{10,8},{14,12},{1,3},{5,7},... | collective-permute-start | bytes 786440 | tf_op jit(solution)/shard_map/ppermute | solution.py:305
  49.3 14.8 %collective-permute-start.4 = (bf16[128,1024]{1,0:T(8,128)(2,1)S(1)}, bf16[128,1024]{1,0:T(8,128)(2,1)S(1)}, u32[]{:S(2)}, u32[]{:S(2)}) collective-permute-start(bf16[128,1024]{1,0:T(8,128)(2,1)S(1)} %slice_select_fusion.refs_4_), channel_id=1, source_target_pairs={{0,2},{4,6},{8,10},{12,14},{2,0},{6,4},{10,8},{14,12},{1,3},{5,7},... | collective-permute-start | bytes 786440 | tf_op jit(solution)/shard_map/ppermute | solution.py:305
  53.3 45.2 %copy-start.4 = (bf16[128,1024]{1,0:T(8,128)(2,1)}, bf16[128,1024]{1,0:T(8,128)(2,1)S(1)}, u32[]{:S(2)}) copy-start(bf16[128,1024]{1,0:T(8,128)(2,1)S(1)} %collective-permute-done.5.refs_7_) | copy-start | bytes 786436
  53.3 16.4 %collective-permute-start.6 = (bf16[128,1024]{1,0:T(8,128)(2,1)S(1)}, bf16[128,1024]{1,0:T(8,128)(2,1)S(1)}, u32[]{:S(2)}, u32[]{:S(2)}) collective-permute-start(bf16[128,1024]{1,0:T(8,128)(2,1)S(1)} %collective-permute-done.5.refs_7_), channel_id=1, source_target_pairs={{0,2},{4,6},{8,10},{12,14},{2,0},{6,4},{10,8},{14,12},{1,3},{5,7},... | collective-permute-start | bytes 786440 | tf_op jit(solution)/shard_map/ppermute | solution.py:305
  56.3 15.4 %collective-permute-start.11 = (bf16[128,1024]{1,0:T(8,128)(2,1)S(1)}, bf16[128,1024]{1,0:T(8,128)(2,1)S(1)}, u32[]{:S(2)}, u32[]{:S(2)}) collective-permute-start(bf16[128,1024]{1,0:T(8,128)(2,1)S(1)} %collective-permute-done.3.refs_5_), channel_id=1, source_target_pairs={{2,4},{6,8},{10,12},{14,0},{4,2},{8,6},{12,10},{0,14},{3,5},{7,9},... | collective-permute-start | bytes 786440 | tf_op jit(solution)/shard_map/ppermute | solution.py:305
  61.0 10.7 %copy-start.5 = (bf16[128,1024]{1,0:T(8,128)(2,1)}, bf16[128,1024]{1,0:T(8,128)(2,1)S(1)}, u32[]{:S(2)}) copy-start(bf16[128,1024]{1,0:T(8,128)(2,1)S(1)} %collective-permute-done.10.refs_12_) | copy-start | bytes 786436
  61.0 12.6 %collective-permute-start.13 = (bf16[128,1024]{1,0:T(8,128)(2,1)S(1)}, bf16[128,1024]{1,0:T(8,128)(2,1)S(1)}, u32[]{:S(2)}, u32[]{:S(2)}) collective-permute-start(bf16[128,1024]{1,0:T(8,128)(2,1)S(1)} %collective-permute-done.10.refs_12_), channel_id=1, source_target_pairs={{2,4},{6,8},{10,12},{14,0},{4,2},{8,6},{12,10},{0,14},{3,5},{7,9},... | collective-permute-start | bytes 786440 | tf_op jit(solution)/shard_map/ppermute | solution.py:305
  64.1 9.5 %copy-start.6 = (bf16[128,1024]{1,0:T(8,128)(2,1)}, bf16[128,1024]{1,0:T(8,128)(2,1)S(1)}, u32[]{:S(2)}) copy-start(bf16[128,1024]{1,0:T(8,128)(2,1)S(1)} %collective-permute-done.4.refs_6_) | copy-start | bytes 786436
  64.1 13.5 %collective-permute-start.7 = (bf16[128,1024]{1,0:T(8,128)(2,1)S(1)}, bf16[128,1024]{1,0:T(8,128)(2,1)}, u32[]{:S(2)}, u32[]{:S(2)}) collective-permute-start(bf16[128,1024]{1,0:T(8,128)(2,1)S(1)} %collective-permute-done.4.refs_6_), channel_id=1, source_target_pairs={{2,4},{6,8},{10,12},{14,0},{4,2},{8,6},{12,10},{0,14},{3,5},{7,9},... | collective-permute-start | bytes 786440 | tf_op jit(solution)/shard_map/ppermute | solution.py:305
  69.7 7.9 %copy-start.7 = (bf16[128,1024]{1,0:T(8,128)(2,1)}, bf16[128,1024]{1,0:T(8,128)(2,1)S(1)}, u32[]{:S(2)}) copy-start(bf16[128,1024]{1,0:T(8,128)(2,1)S(1)} %collective-permute-done.6.refs_8_) | copy-start | bytes 786436
  69.7 10.4 %collective-permute-start.9 = (bf16[128,1024]{1,0:T(8,128)(2,1)S(1)}, bf16[128,1024]{1,0:T(8,128)(2,1)}, u32[]{:S(2)}, u32[]{:S(2)}) collective-permute-start(bf16[128,1024]{1,0:T(8,128)(2,1)S(1)} %collective-permute-done.6.refs_8_), channel_id=1, source_target_pairs={{2,4},{6,8},{10,12},{14,0},{4,2},{8,6},{12,10},{0,14},{3,5},{7,9},... | collective-permute-start | bytes 786440 | tf_op jit(solution)/shard_map/ppermute | solution.py:305
  71.7 8.5 %copy-start.8 = (bf16[128,1024]{1,0:T(8,128)(2,1)}, bf16[128,1024]{1,0:T(8,128)(2,1)S(1)}, u32[]{:S(2)}) copy-start(bf16[128,1024]{1,0:T(8,128)(2,1)S(1)} %collective-permute-done.11.refs_13_) | copy-start | bytes 786436
  71.7 11.8 %collective-permute-start.12 = (bf16[128,1024]{1,0:T(8,128)(2,1)S(1)}, bf16[128,1024]{1,0:T(8,128)(2,1)}, u32[]{:S(2)}, u32[]{:S(2)}) collective-permute-start(bf16[128,1024]{1,0:T(8,128)(2,1)S(1)} %collective-permute-done.11.refs_13_), channel_id=1, source_target_pairs={{0,2},{4,6},{8,10},{12,14},{2,0},{6,4},{10,8},{14,12},{1,3},{5,7},... | collective-permute-start | bytes 786440 | tf_op jit(solution)/shard_map/ppermute | solution.py:305
  73.6 9.9 %copy-start.9 = (bf16[128,1024]{1,0:T(8,128)(2,1)}, bf16[128,1024]{1,0:T(8,128)(2,1)S(1)}, u32[]{:S(2)}) copy-start(bf16[128,1024]{1,0:T(8,128)(2,1)S(1)} %collective-permute-done.13.refs_15_) | copy-start | bytes 786436
  73.6 15.0 %collective-permute-start.14 = (bf16[128,1024]{1,0:T(8,128)(2,1)S(1)}, bf16[128,1024]{1,0:T(8,128)(2,1)}, u32[]{:S(2)}, u32[]{:S(2)}) collective-permute-start(bf16[128,1024]{1,0:T(8,128)(2,1)S(1)} %collective-permute-done.13.refs_15_), channel_id=1, source_target_pairs={{0,2},{4,6},{8,10},{12,14},{2,0},{6,4},{10,8},{14,12},{1,3},{5,7},... | collective-permute-start | bytes 786440 | tf_op jit(solution)/shard_map/ppermute | solution.py:305
  77.6 16.4 %collective-permute-start.8 = (bf16[128,1024]{1,0:T(8,128)(2,1)}, bf16[128,1024]{1,0:T(8,128)(2,1)}, u32[]{:S(2)}, u32[]{:S(2)}) collective-permute-start(bf16[128,1024]{1,0:T(8,128)(2,1)} %collective-permute-done.7.refs_9_), channel_id=1, source_target_pairs={{0,2},{4,6},{8,10},{12,14},{2,0},{6,4},{10,8},{14,12},{1,3},{5,7},... | collective-permute-start | bytes 786440 | tf_op jit(solution)/shard_map/ppermute | solution.py:305
  80.2 13.9 %collective-permute-start.16 = (bf16[128,1024]{1,0:T(8,128)(2,1)}, bf16[128,1024]{1,0:T(8,128)(2,1)}, u32[]{:S(2)}, u32[]{:S(2)}) collective-permute-start(bf16[128,1024]{1,0:T(8,128)(2,1)} %collective-permute-done.9.refs_11_), channel_id=1, source_target_pairs={{0,2},{4,6},{8,10},{12,14},{2,0},{6,4},{10,8},{14,12},{1,3},{5,7},... | collective-permute-start | bytes 786440 | tf_op jit(solution)/shard_map/ppermute | solution.py:305
  83.5 10.6 %collective-permute-start.15 = (bf16[128,1024]{1,0:T(8,128)(2,1)}, bf16[128,1024]{1,0:T(8,128)(2,1)}, u32[]{:S(2)}, u32[]{:S(2)}) collective-permute-start(bf16[128,1024]{1,0:T(8,128)(2,1)} %collective-permute-done.12.refs_14_), channel_id=1, source_target_pairs={{2,4},{6,8},{10,12},{14,0},{4,2},{8,6},{12,10},{0,14},{3,5},{7,9},... | collective-permute-start | bytes 786440 | tf_op jit(solution)/shard_map/ppermute | solution.py:305
  88.6 9.8 %collective-permute-start.17 = (bf16[128,1024]{1,0:T(8,128)(2,1)}, bf16[128,1024]{1,0:T(8,128)(2,1)}, u32[]{:S(2)}, u32[]{:S(2)}) collective-permute-start(bf16[128,1024]{1,0:T(8,128)(2,1)} %collective-permute-done.14.refs_16_), channel_id=1, source_target_pairs={{2,4},{6,8},{10,12},{14,0},{4,2},{8,6},{12,10},{0,14},{3,5},{7,9},... | collective-permute-start | bytes 786440 | tf_op jit(solution)/shard_map/ppermute | solution.py:305

commit v3 on v2

--- a/solution.py
+++ b/solution.py
@@ -131,7 +131,6 @@
 
         for_wanted(lambda copies: copies[half].start())
 
-    for_wanted(lambda copies: copies[0].wait())
     lane = lax.broadcasted_iota(jnp.int32, (1, CHUNK * SPAN), 1)
     rows = QUERIES_PER_KV * SPAN
 
@@ -142,10 +141,14 @@
             end = plan[half, ENDS + doc]
             start = jnp.where(position >= end, end, start)
         chunks = plan[half, CHUNKS]
-        query_copy(half, 0).wait()
         peaks[...] = jnp.full_like(peaks, MASK_FLOOR)
         sums[...] = jnp.zeros_like(sums)
         mixed[...] = jnp.zeros_like(mixed)
+        query_copy(half, 0).wait()
+
+        @pl.when(half == 0)
+        def _():
+            for_wanted(lambda copies: copies[0].wait())
 
         def first_rows(chunk):
             return [
@@ -292,8 +295,8 @@
     kv = resident[:, QUERY_WIDTH:]
     query_odd = trade(resident, 1)
     even_rows = trade(resident, 0)
+    kv_even = trade(kv, 0)
     kv_odd = trade(kv, 1)
-    kv_even = even_rows[:, QUERY_WIDTH:]
     own_sources = lax.dynamic_slice_in_dim(dest[0], 2 * (2 * column + row), 2)
     row_from = jnp.repeat(own_sources, SPAN)[:, None]
     own = jnp.where(
@@ -310,11 +313,14 @@
     for stream in (own, other):
         even, odd_side = stream, stream
         for step in range(1, 4):
-            even, odd_side = across(odd_side, 0), across(even, 1)
+            next_even = across(odd_side, 0)
+            odd_side = across(even, 1)
+            even = next_even
             arrays += [even, odd_side]
             ways += [step, -step]
         last.append((even, odd_side))
-    arrays += [across(last[0][1], 0), across(last[1][0], 1)]
+    arrays.append(across(last[0][1], 0))
+    arrays.append(across(last[1][0], 1))
     ways += [4, 4]
     flips = [0, 1] + [0] * 6 + [1] * 6 + [0, 1]
     pieces = [

time: 107 us -> 111 us (1.037)
  the two profiles are of different devices: /device:TPU:22 before, /device:TPU:16 now
where the time goes in v3:
time: 111 us; the launch traced here: 110 us
  starting transfers between devices  83.9 us (76%)
  waiting for transfers between devices  11.5 us (10%)
  Pallas kernels  9.18 us (8%)
  other arithmetic  2.38 us (2%)
  local copies, waits for them, and re-layouts  2.14 us (2%)
    ppermute x14, starting transfers between devices, across(): return lax.ppermute(array, 'ctx_0', swaps(columns, first))  49.5 us
    ppermute x4, starting transfers between devices, trade(): return lax.ppermute(array, 'dp', swaps(dp_count, first))  31.4 us
    ppermute x14, waiting for transfers between devices, across(): return lax.ppermute(array, 'ctx_0', swaps(columns, first))  7.65 us
    pallas_call x1, Pallas kernels, attention(): pl.pallas_call(functools.partial(attention_kernel, pieces, count), out_sh...  6.93 us
    ppermute x4, waiting for transfers between devices, trade(): return lax.ppermute(array, 'dp', swaps(dp_count, first))  3.85 us
    ppermute x1, starting transfers between devices, on_device(): other = lax.ppermute(own, 'ctx_1', [(0, 1), (1, 0)])  3 us
    pallas_call x1, Pallas kernels, list_key_spans(): pl.pallas_call(functools.partial(list_kernel, pieces), out_shape=jax.Shap...  2.25 us
  transfers between devices with their start and end apart: 19, of which 8 were waited for; matrix products, arithmetic and copies ran while one was open for 2% of the time, Pallas kernels for 2%

profile of v3, /device:TPU:16, one launch (start us, length us, event | category | flops | bytes accessed | tf_op | source)
XLA Modules:
  0.0 109.5 jit_solution(10345130046649254885)
XLA Ops:
  0.0 1.1 slice.4
  1.1 20.2 %collective-permute-start.3 = (bf16[128,1024]{1,0:T(8,128)(2,1)S(1)}, bf16[128,1024]{1,0:T(8,128)(2,1)S(1)}, u32[]{:S(2)}, u32[]{:S(2)}) collective-permute-start(bf16[128,1024]{1,0:T(8,128)(2,1)S(1)} %slice.4), channel_id=1, source_target_pairs={{16,32},{48,64},{80,96},{112,128},{144,160},{176,192},{208,224},{2... | collective-permute-start | bytes 786440 | tf_op jit(solution)/shard_map/ppermute | solution.py:293
  21.3 1.9 %collective-permute-start.2 = (bf16[128,1024]{1,0:T(8,128)(2,1)S(1)}, bf16[128,1024]{1,0:T(8,128)(2,1)S(1)}, u32[]{:S(2)}, u32[]{:S(2)}) collective-permute-start(bf16[128,1024]{1,0:T(8,128)(2,1)S(1)} %slice.4), channel_id=1, source_target_pairs={{0,16},{32,48},{64,80},{96,112},{128,144},{160,176},{192,208},{224... | collective-permute-start | bytes 786440 | tf_op jit(solution)/shard_map/ppermute | solution.py:293
  23.3 0.7 compare_bitcast_fusion.1
  24.0 0.1 broadcast_in_dim.44
  24.1 0.1 eq.57
  24.2 0.1 broadcast_in_dim.46
  24.2 0.1 eq.61
  24.3 3.8 %collective-permute-done.3 = bf16[128,1024]{1,0:T(8,128)(2,1)S(1)} collective-permute-done((bf16[128,1024]{1,0:T(8,128)(2,1)S(1)}, bf16[128,1024]{1,0:T(8,128)(2,1)S(1)}, u32[]{:S(2)}, u32[]{:S(2)}) %collective-permute-start.3) | collective-permute-done | bytes 262176 | tf_op jit(solution)/shard_map/ppermute | solution.py:293
  28.2 0.0 collective-permute-done.2
  28.2 1.1 select_select_fusion.refs_4_
  29.2 4.8 %collective-permute-start.6 = (bf16[128,1024]{1,0:T(8,128)(2,1)S(1)}, bf16[128,1024]{1,0:T(8,128)(2,1)S(1)}, u32[]{:S(2)}, u32[]{:S(2)}) collective-permute-start(bf16[128,1024]{1,0:T(8,128)(2,1)S(1)} %select_select_fusion.refs_4_), channel_id=1, source_target_pairs={{2,4},{6,8},{10,12},{14,0},{4,2},{8,6},{12,10},{0,14},{3,5},{7,9},... | collective-permute-start | bytes 786440 | tf_op jit(solution)/shard_map/ppermute | solution.py:308
  34.0 2.0 %collective-permute-start.5 = (bf16[128,1024]{1,0:T(8,128)(2,1)S(1)}, bf16[128,1024]{1,0:T(8,128)(2,1)S(1)}, u32[]{:S(2)}, u32[]{:S(2)}) collective-permute-start(bf16[128,1024]{1,0:T(8,128)(2,1)S(1)} %select_select_fusion.refs_4_), channel_id=1, source_target_pairs={{0,2},{4,6},{8,10},{12,14},{2,0},{6,4},{10,8},{14,12},{1,3},{5,7},... | collective-permute-start | bytes 786440 | tf_op jit(solution)/shard_map/ppermute | solution.py:308
  36.1 3.0 %collective-permute-start.4 = (bf16[128,1024]{1,0:T(8,128)(2,1)S(1)}, bf16[128,1024]{1,0:T(8,128)(2,1)S(1)}, u32[]{:S(2)}, u32[]{:S(2)}) collective-permute-start(bf16[128,1024]{1,0:T(8,128)(2,1)S(1)} %select_select_fusion.refs_4_), channel_id=1, source_target_pairs={{0,1},{1,0},{2,3},{3,2},{4,5},{5,4},{6,7},{7,6},{8,9},{9,8},{10,11... | collective-permute-start | bytes 786440 | tf_op jit(solution)/shard_map/ppermute | solution.py:305
  39.1 7.3 %collective-permute-start.1 = (bf16[128,5120]{1,0:T(8,128)(2,1)S(1)}, bf16[128,5120]{1,0:T(8,128)(2,1)S(1)}, u32[]{:S(2)}, u32[]{:S(2)}) collective-permute-start(bf16[128,5120]{1,0:T(8,128)(2,1)S(1)} %bitcast.9), channel_id=1, source_target_pairs={{16,32},{48,64},{80,96},{112,128},{144,160},{176,192},{208,224},{2... | collective-permute-start | bytes 3932168 | tf_op jit(solution)/shard_map/ppermute | solution.py:293
  46.4 1.9 %collective-permute-start = (bf16[128,5120]{1,0:T(8,128)(2,1)S(1)}, bf16[128,5120]{1,0:T(8,128)(2,1)}, u32[]{:S(2)}, u32[]{:S(2)}) collective-permute-start(bf16[128,5120]{1,0:T(8,128)(2,1)S(1)} %bitcast.10), channel_id=1, source_target_pairs={{0,16},{32,48},{64,80},{96,112},{128,144},{160,176},{192,208},{224... | collective-permute-start | bytes 3932168 | tf_op jit(solution)/shard_map/ppermute | solution.py:293
  48.4 0.0 collective-permute-done.6.refs_7_
  48.4 3.6 %collective-permute-start.7 = (bf16[128,1024]{1,0:T(8,128)(2,1)S(1)}, bf16[128,1024]{1,0:T(8,128)(2,1)S(1)}, u32[]{:S(2)}, u32[]{:S(2)}) collective-permute-start(bf16[128,1024]{1,0:T(8,128)(2,1)S(1)} %collective-permute-done.6.refs_7_), channel_id=1, source_target_pairs={{0,2},{4,6},{8,10},{12,14},{2,0},{6,4},{10,8},{14,12},{1,3},{5,7},... | collective-permute-start | bytes 786440 | tf_op jit(solution)/shard_map/ppermute | solution.py:308
  52.0 0.0 collective-permute-done.5.refs_6_
  52.0 3.0 %collective-permute-start.8 = (bf16[128,1024]{1,0:T(8,128)(2,1)S(1)}, bf16[128,1024]{1,0:T(8,128)(2,1)S(1)}, u32[]{:S(2)}, u32[]{:S(2)}) collective-permute-start(bf16[128,1024]{1,0:T(8,128)(2,1)S(1)} %collective-permute-done.5.refs_6_), channel_id=1, source_target_pairs={{2,4},{6,8},{10,12},{14,0},{4,2},{8,6},{12,10},{0,14},{3,5},{7,9},... | collective-permute-start | bytes 786440 | tf_op jit(solution)/shard_map/ppermute | solution.py:308
  55.1 0.0 collective-permute-done.4.refs_5_
  55.1 3.3 %collective-permute-start.11 = (bf16[128,1024]{1,0:T(8,128)(2,1)S(1)}, bf16[128,1024]{1,0:T(8,128)(2,1)S(1)}, u32[]{:S(2)}, u32[]{:S(2)}) collective-permute-start(bf16[128,1024]{1,0:T(8,128)(2,1)S(1)} %collective-permute-done.4.refs_5_), channel_id=1, source_target_pairs={{0,2},{4,6},{8,10},{12,14},{2,0},{6,4},{10,8},{14,12},{1,3},{5,7},... | collective-permute-start | bytes 786440 | tf_op jit(solution)/shard_map/ppermute | solution.py:308
  58.5 0.5 collective-permute-done.7.refs_8_
  59.0 4.5 %collective-permute-start.12 = (bf16[128,1024]{1,0:T(8,128)(2,1)S(1)}, bf16[128,1024]{1,0:T(8,128)(2,1)S(1)}, u32[]{:S(2)}, u32[]{:S(2)}) collective-permute-start(bf16[128,1024]{1,0:T(8,128)(2,1)S(1)} %collective-permute-done.4.refs_5_), channel_id=1, source_target_pairs={{2,4},{6,8},{10,12},{14,0},{4,2},{8,6},{12,10},{0,14},{3,5},{7,9},... | collective-permute-start | bytes 786440 | tf_op jit(solution)/shard_map/ppermute | solution.py:308
  63.5 0.1 collective-permute-done.8.refs_9_
  63.6 3.0 %collective-permute-start.10 = (bf16[128,1024]{1,0:T(8,128)(2,1)S(1)}, bf16[128,1024]{1,0:T(8,128)(2,1)}, u32[]{:S(2)}, u32[]{:S(2)}) collective-permute-start(bf16[128,1024]{1,0:T(8,128)(2,1)S(1)} %collective-permute-done.7.refs_8_), channel_id=1, source_target_pairs={{2,4},{6,8},{10,12},{14,0},{4,2},{8,6},{12,10},{0,14},{3,5},{7,9},... | collective-permute-start | bytes 786440 | tf_op jit(solution)/shard_map/ppermute | solution.py:308
  66.6 0.0 collective-permute-done.11.refs_12_
  66.6 4.0 %collective-permute-start.14 = (bf16[128,1024]{1,0:T(8,128)(2,1)S(1)}, bf16[128,1024]{1,0:T(8,128)(2,1)S(1)}, u32[]{:S(2)}, u32[]{:S(2)}) collective-permute-start(bf16[128,1024]{1,0:T(8,128)(2,1)S(1)} %collective-permute-done.11.refs_12_), channel_id=1, source_target_pairs={{2,4},{6,8},{10,12},{14,0},{4,2},{8,6},{12,10},{0,14},{3,5},{7,9},... | collective-permute-start | bytes 786440 | tf_op jit(solution)/shard_map/ppermute | solution.py:308
  70.7 0.5 collective-permute-done.12.refs_13_
  71.2 3.2 %collective-permute-start.9 = (bf16[128,1024]{1,0:T(8,128)(2,1)S(1)}, bf16[128,1024]{1,0:T(8,128)(2,1)S(1)}, u32[]{:S(2)}, u32[]{:S(2)}) collective-permute-start(bf16[128,1024]{1,0:T(8,128)(2,1)S(1)} %collective-permute-done.8.refs_9_), channel_id=1, source_target_pairs={{0,2},{4,6},{8,10},{12,14},{2,0},{6,4},{10,8},{14,12},{1,3},{5,7},... | collective-permute-start | bytes 786440 | tf_op jit(solution)/shard_map/ppermute | solution.py:308
  74.4 2.5 %collective-permute-done.10.refs_11_ = bf16[128,1024]{1,0:T(8,128)(2,1)} collective-permute-done((bf16[128,1024]{1,0:T(8,128)(2,1)S(1)}, bf16[128,1024]{1,0:T(8,128)(2,1)}, u32[]{:S(2)}, u32[]{:S(2)}) %collective-permute-start.10) | collective-permute-done | bytes 262176 | tf_op jit(solution)/shard_map/ppermute | solution.py:308
  76.9 3.2 %collective-permute-start.13 = (bf16[128,1024]{1,0:T(8,128)(2,1)S(1)}, bf16[128,1024]{1,0:T(8,128)(2,1)}, u32[]{:S(2)}, u32[]{:S(2)}) collective-permute-start(bf16[128,1024]{1,0:T(8,128)(2,1)S(1)} %collective-permute-done.12.refs_13_), channel_id=1, source_target_pairs={{0,2},{4,6},{8,10},{12,14},{2,0},{6,4},{10,8},{14,12},{1,3},{5,7},... | collective-permute-start | bytes 786440 | tf_op jit(solution)/shard_map/ppermute | solution.py:308
  80.1 1.0 collective-permute-done.14.refs_15_
  81.2 3.0 %collective-permute-start.15 = (bf16[128,1024]{1,0:T(8,128)(2,1)S(1)}, bf16[128,1024]{1,0:T(8,128)(2,1)}, u32[]{:S(2)}, u32[]{:S(2)}) collective-permute-start(bf16[128,1024]{1,0:T(8,128)(2,1)S(1)} %collective-permute-done.14.refs_15_), channel_id=1, source_target_pairs={{0,2},{4,6},{8,10},{12,14},{2,0},{6,4},{10,8},{14,12},{1,3},{5,7},... | collective-permute-start | bytes 786440 | tf_op jit(solution)/shard_map/ppermute | solution.py:308
  84.1 0.0 collective-permute-done.9.refs_10_
  84.2 2.9 %collective-permute-start.17 = (bf16[128,1024]{1,0:T(8,128)(2,1)}, bf16[128,1024]{1,0:T(8,128)(2,1)}, u32[]{:S(2)}, u32[]{:S(2)}) collective-permute-start(bf16[128,1024]{1,0:T(8,128)(2,1)} %collective-permute-done.10.refs_11_), channel_id=1, source_target_pairs={{0,2},{4,6},{8,10},{12,14},{2,0},{6,4},{10,8},{14,12},{1,3},{5,7},... | collective-permute-start | bytes 786440 | tf_op jit(solution)/shard_map/ppermute | solution.py:308
  87.1 0.0 collective-permute-done.13.refs_14_
  87.1 4.5 %collective-permute-start.16 = (bf16[128,1024]{1,0:T(8,128)(2,1)}, bf16[128,1024]{1,0:T(8,128)(2,1)}, u32[]{:S(2)}, u32[]{:S(2)}) collective-permute-start(bf16[128,1024]{1,0:T(8,128)(2,1)} %collective-permute-done.13.refs_14_), channel_id=1, source_target_pairs={{2,4},{6,8},{10,12},{14,0},{4,2},{8,6},{12,10},{0,14},{3,5},{7,9},... | collective-permute-start | bytes 786440 | tf_op jit(solution)/shard_map/ppermute | solution.py:308
  91.6 0.8 collective-permute-done.15.refs_16_
  92.3 4.5 %collective-permute-start.18 = (bf16[128,1024]{1,0:T(8,128)(2,1)}, bf16[128,1024]{1,0:T(8,128)(2,1)}, u32[]{:S(2)}, u32[]{:S(2)}) collective-permute-start(bf16[128,1024]{1,0:T(8,128)(2,1)} %collective-permute-done.15.refs_16_), channel_id=1, source_target_pairs={{2,4},{6,8},{10,12},{14,0},{4,2},{8,6},{12,10},{0,14},{3,5},{7,9},... | collective-permute-start | bytes 786440 | tf_op jit(solution)/shard_map/ppermute | solution.py:308
  96.8 0.7 copy.5.lengths_ref
  97.5 0.6 compare_select_fusion.3.where_ref
  98.1 2.2 %list_spans.1.refs_0_ = s32[2,128]{1,0:T(2,128)} custom-call(s32[8]{0:T(128)} %compare_select_fusion.3.where_ref, s32[1,32]{1,0:T(1,128)} %dest_ref.1, s32[32]{0:T(128)} %order_ref.1, s32[64,8]{1,0:T(8,128)} %copy.5.lengths_ref), custom_call_target="tpu_custom_call" | custom-call | flops 4000000 | bytes 4000 | tf_op jit(solution)/shard_map/list_spans/pallas_call | solution.py:236
  100.4 0.0 collective-permute-done.17.refs_18_
  100.4 0.0 collective-permute-done.16.refs_17_
  100.4 0.0 collective-permute-done.1.refs_3_
  100.4 2.2 %collective-permute-done.18.refs_19_ = bf16[128,1024]{1,0:T(8,128)(2,1)} collective-permute-done((bf16[128,1024]{1,0:T(8,128)(2,1)}, bf16[128,1024]{1,0:T(8,128)(2,1)}, u32[]{:S(2)}, u32[]{:S(2)}) %collective-permute-start.18) | collective-permute-done | bytes 262176 | tf_op jit(solution)/shard_map/ppermute | solution.py:308
  102.6 6.9 %attend.1 = bf16[128,4096]{1,0:T(8,128)(2,1)} custom-call(s32[2,128]{1,0:T(2,128)} %list_spans.1.refs_0_, bf16[128,5120]{1,0:T(8,128)(2,1)} %bitcast.8, bf16[128,5120]{1,0:T(8,128)(2,1)} %collective-permute-done.refs_2_, bf16[128,5120]{1,0:T(8,128)(2,1)} %copy-done.1, bf16[128,1024]{1,0:T(8,128)(2,1)} %copy-done.2, bf16[128,1024]{1,0:T(8,128)(2,1)} %copy-done.5, ...), custom_call_target="tpu_custom_call" | custom-call | flops 1000000000 | bytes 4000000 | tf_op jit(solution)/shard_map/attend/pallas_call | solution.py:251
  (27 shorter events, 0.1 us)
Async XLA Ops:
  0.0 39.1 %copy-start = (bf16[1,128,5120]{2,1,0:T(8,128)(2,1)S(1)}, bf16[1,128,5120]{2,1,0:T(8,128)(2,1)}, u32[]{:S(2)}) copy-start(bf16[1,128,5120]{2,1,0:T(8,128)(2,1)} %param.4) | copy-start | bytes 3932164
  0.0 96.8 %copy-start.12 = (s32[64,8]{0,1:T(8,128)S(1)}, s32[64,8]{0,1:T(8,128)}, u32[]{:S(2)}) copy-start(s32[64,8]{0,1:T(8,128)} %param.7) | copy-start | bytes 6148
  1.1 27.1 %collective-permute-start.3 = (bf16[128,1024]{1,0:T(8,128)(2,1)S(1)}, bf16[128,1024]{1,0:T(8,128)(2,1)S(1)}, u32[]{:S(2)}, u32[]{:S(2)}) collective-permute-start(bf16[128,1024]{1,0:T(8,128)(2,1)S(1)} %slice.4), channel_id=1, source_target_pairs={{16,32},{48,64},{80,96},{112,128},{144,160},{176,192},{208,224},{2... | collective-permute-start | bytes 786440 | tf_op jit(solution)/shard_map/ppermute | solution.py:293
  21.3 6.9 %collective-permute-start.2 = (bf16[128,1024]{1,0:T(8,128)(2,1)S(1)}, bf16[128,1024]{1,0:T(8,128)(2,1)S(1)}, u32[]{:S(2)}, u32[]{:S(2)}) collective-permute-start(bf16[128,1024]{1,0:T(8,128)(2,1)S(1)} %slice.4), channel_id=1, source_target_pairs={{0,16},{32,48},{64,80},{96,112},{128,144},{160,176},{192,208},{224... | collective-permute-start | bytes 786440 | tf_op jit(solution)/shard_map/ppermute | solution.py:293
  29.2 73.4 %copy-start.2 = (bf16[128,1024]{1,0:T(8,128)(2,1)}, bf16[128,1024]{1,0:T(8,128)(2,1)S(1)}, u32[]{:S(2)}) copy-start(bf16[128,1024]{1,0:T(8,128)(2,1)S(1)} %select_select_fusion.refs_4_) | copy-start | bytes 786436
  29.2 19.1 %collective-permute-start.6 = (bf16[128,1024]{1,0:T(8,128)(2,1)S(1)}, bf16[128,1024]{1,0:T(8,128)(2,1)S(1)}, u32[]{:S(2)}, u32[]{:S(2)}) collective-permute-start(bf16[128,1024]{1,0:T(8,128)(2,1)S(1)} %select_select_fusion.refs_4_), channel_id=1, source_target_pairs={{2,4},{6,8},{10,12},{14,0},{4,2},{8,6},{12,10},{0,14},{3,5},{7,9},... | collective-permute-start | bytes 786440 | tf_op jit(solution)/shard_map/ppermute | solution.py:308
  34.0 18.0 %collective-permute-start.5 = (bf16[128,1024]{1,0:T(8,128)(2,1)S(1)}, bf16[128,1024]{1,0:T(8,128)(2,1)S(1)}, u32[]{:S(2)}, u32[]{:S(2)}) collective-permute-start(bf16[128,1024]{1,0:T(8,128)(2,1)S(1)} %select_select_fusion.refs_4_), channel_id=1, source_target_pairs={{0,2},{4,6},{8,10},{12,14},{2,0},{6,4},{10,8},{14,12},{1,3},{5,7},... | collective-permute-start | bytes 786440 | tf_op jit(solution)/shard_map/ppermute | solution.py:308
  36.1 19.0 %collective-permute-start.4 = (bf16[128,1024]{1,0:T(8,128)(2,1)S(1)}, bf16[128,1024]{1,0:T(8,128)(2,1)S(1)}, u32[]{:S(2)}, u32[]{:S(2)}) collective-permute-start(bf16[128,1024]{1,0:T(8,128)(2,1)S(1)} %select_select_fusion.refs_4_), channel_id=1, source_target_pairs={{0,1},{1,0},{2,3},{3,2},{4,5},{5,4},{6,7},{7,6},{8,9},{9,8},{10,11... | collective-permute-start | bytes 786440 | tf_op jit(solution)/shard_map/ppermute | solution.py:305
  39.1 61.3 %collective-permute-start.1 = (bf16[128,5120]{1,0:T(8,128)(2,1)S(1)}, bf16[128,5120]{1,0:T(8,128)(2,1)S(1)}, u32[]{:S(2)}, u32[]{:S(2)}) collective-permute-start(bf16[128,5120]{1,0:T(8,128)(2,1)S(1)} %bitcast.9), channel_id=1, source_target_pairs={{16,32},{48,64},{80,96},{112,128},{144,160},{176,192},{208,224},{2... | collective-permute-start | bytes 3932168 | tf_op jit(solution)/shard_map/ppermute | solution.py:293
  46.4 54.0 %collective-permute-start = (bf16[128,5120]{1,0:T(8,128)(2,1)S(1)}, bf16[128,5120]{1,0:T(8,128)(2,1)}, u32[]{:S(2)}, u32[]{:S(2)}) collective-permute-start(bf16[128,5120]{1,0:T(8,128)(2,1)S(1)} %bitcast.10), channel_id=1, source_target_pairs={{0,16},{32,48},{64,80},{96,112},{128,144},{160,176},{192,208},{224... | collective-permute-start | bytes 3932168 | tf_op jit(solution)/shard_map/ppermute | solution.py:293
  48.4 54.2 %copy-start.3 = (bf16[128,1024]{1,0:T(8,128)(2,1)}, bf16[128,1024]{1,0:T(8,128)(2,1)S(1)}, u32[]{:S(2)}) copy-start(bf16[128,1024]{1,0:T(8,128)(2,1)S(1)} %collective-permute-done.6.refs_7_) | copy-start | bytes 786436
  48.4 10.6 %collective-permute-start.7 = (bf16[128,1024]{1,0:T(8,128)(2,1)S(1)}, bf16[128,1024]{1,0:T(8,128)(2,1)S(1)}, u32[]{:S(2)}, u32[]{:S(2)}) collective-permute-start(bf16[128,1024]{1,0:T(8,128)(2,1)S(1)} %collective-permute-done.6.refs_7_), channel_id=1, source_target_pairs={{0,2},{4,6},{8,10},{12,14},{2,0},{6,4},{10,8},{14,12},{1,3},{5,7},... | collective-permute-start | bytes 786440 | tf_op jit(solution)/shard_map/ppermute | solution.py:308
  52.0 50.6 %copy-start.4 = (bf16[128,1024]{1,0:T(8,128)(2,1)}, bf16[128,1024]{1,0:T(8,128)(2,1)S(1)}, u32[]{:S(2)}) copy-start(bf16[128,1024]{1,0:T(8,128)(2,1)S(1)} %collective-permute-done.5.refs_6_) | copy-start | bytes 786436
  52.0 11.5 %collective-permute-start.8 = (bf16[128,1024]{1,0:T(8,128)(2,1)S(1)}, bf16[128,1024]{1,0:T(8,128)(2,1)S(1)}, u32[]{:S(2)}, u32[]{:S(2)}) collective-permute-start(bf16[128,1024]{1,0:T(8,128)(2,1)S(1)} %collective-permute-done.5.refs_6_), channel_id=1, source_target_pairs={{2,4},{6,8},{10,12},{14,0},{4,2},{8,6},{12,10},{0,14},{3,5},{7,9},... | collective-permute-start | bytes 786440 | tf_op jit(solution)/shard_map/ppermute | solution.py:308
  55.1 8.5 %copy-start.5 = (bf16[128,1024]{1,0:T(8,128)(2,1)}, bf16[128,1024]{1,0:T(8,128)(2,1)S(1)}, u32[]{:S(2)}) copy-start(bf16[128,1024]{1,0:T(8,128)(2,1)S(1)} %collective-permute-done.4.refs_5_) | copy-start | bytes 786436
  55.1 11.5 %collective-permute-start.11 = (bf16[128,1024]{1,0:T(8,128)(2,1)S(1)}, bf16[128,1024]{1,0:T(8,128)(2,1)S(1)}, u32[]{:S(2)}, u32[]{:S(2)}) collective-permute-start(bf16[128,1024]{1,0:T(8,128)(2,1)S(1)} %collective-permute-done.4.refs_5_), channel_id=1, source_target_pairs={{0,2},{4,6},{8,10},{12,14},{2,0},{6,4},{10,8},{14,12},{1,3},{5,7},... | collective-permute-start | bytes 786440 | tf_op jit(solution)/shard_map/ppermute | solution.py:308
  59.0 12.2 %copy-start.6 = (bf16[128,1024]{1,0:T(8,128)(2,1)}, bf16[128,1024]{1,0:T(8,128)(2,1)S(1)}, u32[]{:S(2)}) copy-start(bf16[128,1024]{1,0:T(8,128)(2,1)S(1)} %collective-permute-done.7.refs_8_) | copy-start | bytes 786436
  59.0 12.2 %collective-permute-start.12 = (bf16[128,1024]{1,0:T(8,128)(2,1)S(1)}, bf16[128,1024]{1,0:T(8,128)(2,1)S(1)}, u32[]{:S(2)}, u32[]{:S(2)}) collective-permute-start(bf16[128,1024]{1,0:T(8,128)(2,1)S(1)} %collective-permute-done.4.refs_5_), channel_id=1, source_target_pairs={{2,4},{6,8},{10,12},{14,0},{4,2},{8,6},{12,10},{0,14},{3,5},{7,9},... | collective-permute-start | bytes 786440 | tf_op jit(solution)/shard_map/ppermute | solution.py:308
  63.6 13.4 %copy-start.7 = (bf16[128,1024]{1,0:T(8,128)(2,1)}, bf16[128,1024]{1,0:T(8,128)(2,1)S(1)}, u32[]{:S(2)}) copy-start(bf16[128,1024]{1,0:T(8,128)(2,1)S(1)} %collective-permute-done.8.refs_9_) | copy-start | bytes 786436
  63.6 13.3 %collective-permute-start.10 = (bf16[128,1024]{1,0:T(8,128)(2,1)S(1)}, bf16[128,1024]{1,0:T(8,128)(2,1)}, u32[]{:S(2)}, u32[]{:S(2)}) collective-permute-start(bf16[128,1024]{1,0:T(8,128)(2,1)S(1)} %collective-permute-done.7.refs_8_), channel_id=1, source_target_pairs={{2,4},{6,8},{10,12},{14,0},{4,2},{8,6},{12,10},{0,14},{3,5},{7,9},... | collective-permute-start | bytes 786440 | tf_op jit(solution)/shard_map/ppermute | solution.py:308
  66.6 17.5 %copy-start.8 = (bf16[128,1024]{1,0:T(8,128)(2,1)}, bf16[128,1024]{1,0:T(8,128)(2,1)S(1)}, u32[]{:S(2)}) copy-start(bf16[128,1024]{1,0:T(8,128)(2,1)S(1)} %collective-permute-done.11.refs_12_) | copy-start | bytes 786436
  66.6 14.5 %collective-permute-start.14 = (bf16[128,1024]{1,0:T(8,128)(2,1)S(1)}, bf16[128,1024]{1,0:T(8,128)(2,1)S(1)}, u32[]{:S(2)}, u32[]{:S(2)}) collective-permute-start(bf16[128,1024]{1,0:T(8,128)(2,1)S(1)} %collective-permute-done.11.refs_12_), channel_id=1, source_target_pairs={{2,4},{6,8},{10,12},{14,0},{4,2},{8,6},{12,10},{0,14},{3,5},{7,9},... | collective-permute-start | bytes 786440 | tf_op jit(solution)/shard_map/ppermute | solution.py:308
  71.2 15.8 %copy-start.9 = (bf16[128,1024]{1,0:T(8,128)(2,1)}, bf16[128,1024]{1,0:T(8,128)(2,1)S(1)}, u32[]{:S(2)}) copy-start(bf16[128,1024]{1,0:T(8,128)(2,1)S(1)} %collective-permute-done.12.refs_13_) | copy-start | bytes 786436
  71.2 12.9 %collective-permute-start.9 = (bf16[128,1024]{1,0:T(8,128)(2,1)S(1)}, bf16[128,1024]{1,0:T(8,128)(2,1)S(1)}, u32[]{:S(2)}, u32[]{:S(2)}) collective-permute-start(bf16[128,1024]{1,0:T(8,128)(2,1)S(1)} %collective-permute-done.8.refs_9_), channel_id=1, source_target_pairs={{0,2},{4,6},{8,10},{12,14},{2,0},{6,4},{10,8},{14,12},{1,3},{5,7},... | collective-permute-start | bytes 786440 | tf_op jit(solution)/shard_map/ppermute | solution.py:308
  76.9 10.1 %collective-permute-start.13 = (bf16[128,1024]{1,0:T(8,128)(2,1)S(1)}, bf16[128,1024]{1,0:T(8,128)(2,1)}, u32[]{:S(2)}, u32[]{:S(2)}) collective-permute-start(bf16[128,1024]{1,0:T(8,128)(2,1)S(1)} %collective-permute-done.12.refs_13_), channel_id=1, source_target_pairs={{0,2},{4,6},{8,10},{12,14},{2,0},{6,4},{10,8},{14,12},{1,3},{5,7},... | collective-permute-start | bytes 786440 | tf_op jit(solution)/shard_map/ppermute | solution.py:308
  81.2 5.9 %copy-start.10 = (bf16[128,1024]{1,0:T(8,128)(2,1)}, bf16[128,1024]{1,0:T(8,128)(2,1)S(1)}, u32[]{:S(2)}) copy-start(bf16[128,1024]{1,0:T(8,128)(2,1)S(1)} %collective-permute-done.14.refs_15_) | copy-start | bytes 786436
  81.2 11.2 %collective-permute-start.15 = (bf16[128,1024]{1,0:T(8,128)(2,1)S(1)}, bf16[128,1024]{1,0:T(8,128)(2,1)}, u32[]{:S(2)}, u32[]{:S(2)}) collective-permute-start(bf16[128,1024]{1,0:T(8,128)(2,1)S(1)} %collective-permute-done.14.refs_15_), channel_id=1, source_target_pairs={{0,2},{4,6},{8,10},{12,14},{2,0},{6,4},{10,8},{14,12},{1,3},{5,7},... | collective-permute-start | bytes 786440 | tf_op jit(solution)/shard_map/ppermute | solution.py:308
  84.2 8.2 %copy-start.11 = (bf16[128,1024]{1,0:T(8,128)(2,1)}, bf16[128,1024]{1,0:T(8,128)(2,1)S(1)}, u32[]{:S(2)}) copy-start(bf16[128,1024]{1,0:T(8,128)(2,1)S(1)} %collective-permute-done.9.refs_10_) | copy-start | bytes 786436
  84.2 16.2 %collective-permute-start.17 = (bf16[128,1024]{1,0:T(8,128)(2,1)}, bf16[128,1024]{1,0:T(8,128)(2,1)}, u32[]{:S(2)}, u32[]{:S(2)}) collective-permute-start(bf16[128,1024]{1,0:T(8,128)(2,1)} %collective-permute-done.10.refs_11_), channel_id=1, source_target_pairs={{0,2},{4,6},{8,10},{12,14},{2,0},{6,4},{10,8},{14,12},{1,3},{5,7},... | collective-permute-start | bytes 786440 | tf_op jit(solution)/shard_map/ppermute | solution.py:308
  87.1 13.3 %collective-permute-start.16 = (bf16[128,1024]{1,0:T(8,128)(2,1)}, bf16[128,1024]{1,0:T(8,128)(2,1)}, u32[]{:S(2)}, u32[]{:S(2)}) collective-permute-start(bf16[128,1024]{1,0:T(8,128)(2,1)} %collective-permute-done.13.refs_14_), channel_id=1, source_target_pairs={{2,4},{6,8},{10,12},{14,0},{4,2},{8,6},{12,10},{0,14},{3,5},{7,9},... | collective-permute-start | bytes 786440 | tf_op jit(solution)/shard_map/ppermute | solution.py:308
  92.3 10.3 %collective-permute-start.18 = (bf16[128,1024]{1,0:T(8,128)(2,1)}, bf16[128,1024]{1,0:T(8,128)(2,1)}, u32[]{:S(2)}, u32[]{:S(2)}) collective-permute-start(bf16[128,1024]{1,0:T(8,128)(2,1)} %collective-permute-done.15.refs_16_), channel_id=1, source_target_pairs={{2,4},{6,8},{10,12},{14,0},{4,2},{8,6},{12,10},{0,14},{3,5},{7,9},... | collective-permute-start | bytes 786440 | tf_op jit(solution)/shard_map/ppermute | solution.py:308
  100.4 2.2 %copy-start.1 = (bf16[128,5120]{1,0:T(8,128)(2,1)}, bf16[128,5120]{1,0:T(8,128)(2,1)S(1)}, u32[]{:S(2)}) copy-start(bf16[128,5120]{1,0:T(8,128)(2,1)S(1)} %collective-permute-done.1.refs_3_) | copy-start | bytes 3932164
